TPU v7x, 256 devices: a whole 4x4x8 slice. The times are simulated.
256 devices in a mesh: batch: 8 (over z), mp: 32 (over x, y, core).
Axes of the slice: x: 4, y: 4, z: 8, core: 2. Of those that a mesh axis runs over, the one named last changes fastest.
Arguments:
- stream: bfloat16 [256, 8192], P(None, 'mp'), may hold values from -6 to 6
- input_gain: float32 [8192], P('mp'), may hold values from 0.5 to 1.5
- query_bias: float32 [8192], P('batch'), may hold values from -3 to 3
- query_weight: bfloat16 [8192, 8192], P('mp', 'batch'), may hold values from -0.0625 to 0.0625
- out_weight: bfloat16 [8192, 8192], P('batch', 'mp'), may hold values from -6 to 6
- page_cache: bfloat16 [2, 8, 2048, 128, 128], P(None, 'batch', 'mp'), may hold values from -43 to 43
- page_table: int32 [256, 24], P('mp'), may hold values from 0 to 63, as said below
- lengths: int32 [256], P('mp'), may hold values from 1 to 3072, as said below
- final_gain: float32 [8192], P('mp'), may hold values from 0.5 to 1.5
- head_weight: bfloat16 [8192, 98304], P('mp', 'batch'), may hold values from -11 to 11
Outputs:
- logits: float32 [256, 98304], P(None, ('batch', 'mp'))
- log_norm: float32 [256], replicated
Inputs may be any that keep to these rules, and one draw needn't show every extreme that they name: Each sequence's pages are the first ceil(lengths / 128) entries of its row of page_table; together the sequences of one index of mp use at most 64 pages; some sequence holds exactly 3072 tokens. `page_table`: entries are slots of the pool of the index of mp that holds the sequence; the live entries (the first ceil(lengths / 128) of each row) of all rows of one index of mp are distinct; later entries are arbitrary slots.
All inputs are finite; a program needn't handle non-finite values.
Results may differ from a plain program's by a relative error of at most 0.0099.
Values may be sent and summed in bfloat16 or wider, within the bound.
No kernel may reach another device: no remote copies, remote signals or barrier semaphores. Data moves between devices by JAX's collectives and lax.ppermute only.
A program may use at most 128 MiB of HBM per device.

v0:
```python
import math

import jax
import jax.numpy as jnp
from jax import lax
from jax.experimental import pallas as pl
from jax.experimental.pallas import tpu as pltpu
from jax.sharding import Mesh
from jax.sharding import PartitionSpec as P

MP = ("mp_0", "mp_1", "mp_2")
BATCH_MP = ("batch", "mp_0", "mp_1", "mp_2")
XY = ("mp_0", "mp_1")
BATCH_CORE = ("batch", "mp_2")


EPS = 1e-06
ROPE_BASE = 1000000.0
INTERPRET = False

LANES = 128


def sent_to_all(x, axis):
    length = lax.axis_size(axis)
    return lax.all_to_all(jnp.broadcast_to(x[None], (length, *x.shape)), axis, 0, 0, tiled=True)


def shifted(x, axis, by):
    length = lax.axis_size(axis)
    return lax.ppermute(x, axis, [(k, (k + by) % length) for k in range(length)])


def halves(x):
    coarse = lax.reduce_precision(x, 8, 7)
    return coarse.astype(jnp.bfloat16), (x - coarse).astype(jnp.bfloat16)


def with_squares(values, squares):
    coarse, fine = halves(squares)
    filler = jnp.zeros((*squares.shape, LANES - 2), jnp.bfloat16)
    return jnp.concatenate(
        [values.astype(jnp.bfloat16), coarse[..., None], fine[..., None], filler], axis=-1
    )


def without_squares(x):
    width = x.shape[-1] - LANES
    tail = x[..., width : width + 2].astype(jnp.float32)
    return x[..., :width], tail[..., 0] + tail[..., 1]


def rotate(queries, position):
    head_size = queries.shape[-1]
    half_dim = head_size // 2
    exponent = jnp.arange(half_dim, dtype=jnp.float32) * (-2.0 / head_size)
    frequency = ROPE_BASE**exponent
    angles = position.astype(jnp.float32)[:, None] * frequency[None, :]
    cosines = jnp.cos(angles)[:, None, :]
    sines = jnp.sin(angles)[:, None, :]
    leading = queries[..., :half_dim]
    trailing = queries[..., half_dim:]
    return jnp.concatenate(
        [leading * cosines - trailing * sines, trailing * cosines + leading * sines], axis=-1
    )


def attend_slots(queries, page_cache, page_table, lengths):
    seq_count, max_pages = page_table.shape
    local_heads, pool_size, page_size, head_size = (
        page_cache.shape[1],
        page_cache.shape[2],
        page_cache.shape[3],
        page_cache.shape[4],
    )
    per_group = queries.shape[1] // local_heads
    used_pages = (lengths + page_size - 1) // page_size
    slot_ids = jnp.arange(pool_size, dtype=jnp.int32)
    page_order = jnp.arange(max_pages, dtype=jnp.int32)
    matches = (page_table[:, :, None] == slot_ids[None, None, :]) & (
        page_order[None, :, None] < used_pages[:, None, None]
    )
    ownership = jnp.any(matches, axis=1)
    page_rank = jnp.sum(jnp.where(matches, page_order[None, :, None], 0), axis=(0, 1))
    length_cap = jnp.sum(jnp.where(ownership, lengths[:, None], 0), axis=0)
    has_owner = jnp.any(ownership, axis=0)
    position = page_rank[:, None] * page_size + jnp.arange(page_size, dtype=jnp.int32)[None, :]
    visible = (position < length_cap[:, None])[None, :, None, :]
    owner_mask = ownership.astype(jnp.bfloat16)
    slot_query = jnp.dot(
        owner_mask.T, queries.reshape(seq_count, -1), preferred_element_type=jnp.float32
    ).astype(jnp.bfloat16)
    slot_query = slot_query.reshape(pool_size, local_heads, per_group, head_size)
    scores = jnp.einsum(
        "phgd,hprd->hpgr", slot_query, page_cache[0], preferred_element_type=jnp.float32
    ) / math.sqrt(head_size)
    scores = jnp.where(visible, scores, -1e30)
    slot_top = jnp.max(scores, axis=3)
    owner_grid = ownership.T[None, :, None, :]
    seq_top = jnp.max(jnp.where(owner_grid, slot_top[..., None], -1e30), axis=1)
    top_slot = jnp.sum(jnp.where(owner_grid, seq_top[:, None, :, :], 0.0), axis=3)
    powers = jnp.where(visible, jnp.exp(scores - top_slot[..., None]), 0.0)
    slot_sum = jnp.sum(powers, axis=3)
    seq_sum = jnp.sum(jnp.where(owner_grid, slot_sum[..., None], 0.0), axis=1)
    sum_slot = jnp.sum(jnp.where(owner_grid, seq_sum[:, None, :, :], 0.0), axis=3)
    divisor = jnp.where(has_owner[None, :, None], sum_slot, 1.0)
    weights = (powers / divisor[..., None]).astype(jnp.bfloat16)
    slot_out = jnp.einsum(
        "hpgr,hprd->phgd", weights, page_cache[1], preferred_element_type=jnp.float32
    )
    result = jnp.dot(
        ownership.astype(jnp.float32),
        slot_out.reshape(pool_size, -1),
        precision=lax.Precision.HIGHEST,
    )
    return result.astype(jnp.bfloat16)


def head_block(place, near, far, *refs):
    side = len(refs) // 4
    near_weights, far_weights = refs[:side], refs[side : 2 * side]
    by_x, by_y = refs[2 * side : 3 * side], refs[3 * side :]
    step = pl.program_id(0)
    half = near.shape[0] // 2
    for k in range(side):
        product = jnp.dot(near[...], near_weights[k][...], preferred_element_type=jnp.float32)
        product += jnp.dot(far[...], far_weights[k][...], preferred_element_type=jnp.float32)
        product = product.astype(jnp.bfloat16)
        by_y[k][0] = product[half:]
        for x_step in range(side):

            @pl.when(step == x_step)
            def _(k=k, x_step=x_step, product=product):
                by_x[x_step][k] = product[:half]


def head_partials(near, far, near_weight, far_weight, x_at, y_at, core_at, side, cores):
    rows, depth = near.shape
    width = near_weight.shape[1] // (side * side * cores)
    half = rows // 2

    def weight_block(k):
        def at(s, place):
            x_to = (place[0] + s) % side
            y_to = (place[1] + k) % side
            return (0, (x_to * side + y_to) * cores + place[2])

        return pl.BlockSpec((depth, width), at)

    out_specs = [pl.BlockSpec((side, half, width), lambda s, place: (0, 0, 0))] * side
    out_specs += [pl.BlockSpec((1, half, width), lambda s, place: (s, 0, 0))] * side
    whole = pl.BlockSpec((rows, depth), lambda s, place: (0, 0))
    weights = [weight_block(k) for k in range(side)]
    outs = pl.pallas_call(
        head_block,
        grid_spec=pltpu.PrefetchScalarGridSpec(
            num_scalar_prefetch=1,
            grid=(side,),
            in_specs=[whole, whole, *weights, *weights],
            out_specs=out_specs,
        ),
        out_shape=[jax.ShapeDtypeStruct((side, half, width), jnp.bfloat16)] * (2 * side),
        compiler_params=pltpu.CompilerParams(dimension_semantics=("arbitrary",)),
        interpret=INTERPRET,
        name="head_partials",
    )(
        jnp.stack([x_at, y_at, core_at]).astype(jnp.int32),
        near,
        far,
        *[near_weight] * side,
        *[far_weight] * side,
    )
    return outs[:side], outs[side:]


def summed_along(parts, axis):
    arrived = [shifted(parts[k], axis, k) for k in range(1, len(parts))]
    total = parts[0].astype(jnp.float32)
    for piece in arrived:
        total = total + piece.astype(jnp.float32)
    return total


def joined_all(top, total, axes):
    for axis in axes:
        pieces = sent_to_all(jnp.stack([top, total]), axis)
        tops = pieces[:, 0]
        top = jnp.max(tops, axis=0)
        total = jnp.sum(pieces[:, 1] * jnp.exp(tops - top[None]), axis=0)
    return top, total


def local(
    stream,
    input_gain,
    query_bias,
    query_weight,
    out_weight,
    page_cache,
    page_table,
    lengths,
    final_gain,
    head_weight,
):
    side, cores, batches = lax.axis_size("mp_0"), lax.axis_size("mp_2"), lax.axis_size("batch")
    members = side * side * cores
    x_at, y_at, core_at = lax.axis_index("mp_0"), lax.axis_index("mp_1"), lax.axis_index("mp_2")
    batch_at = lax.axis_index("batch")
    first_core = core_at == 0
    seqs, features_here = stream.shape
    full_width = features_here * members
    seq_count = page_table.shape[0]
    head_size = page_cache.shape[-1]

    far_head_weight = shifted(head_weight, "mp_2", 1)
    far_out_weight = shifted(out_weight, "mp_2", 1)

    features = stream.astype(jnp.float32)
    scaled = (features * input_gain).astype(jnp.bfloat16)
    products = jnp.dot(scaled, query_weight, preferred_element_type=jnp.float32)
    payload = with_squares(products, jnp.sum(features * features, axis=1))
    arrived = lax.all_to_all(
        payload.reshape(members, seq_count, -1), MP, split_axis=0, concat_axis=0, tiled=True
    )
    products, squares = without_squares(arrived)
    scale = lax.rsqrt(jnp.sum(squares, axis=0) / full_width + EPS)
    queries = jnp.sum(products.astype(jnp.float32), axis=0) * scale[:, None] + query_bias
    queries = rotate(queries.reshape(seq_count, -1, head_size), lengths - 1).astype(jnp.bfloat16)
    attended = attend_slots(queries, page_cache, page_table, lengths)

    mine = sent_to_all(attended, XY).reshape(side * side * seq_count, -1)
    near_out = jnp.dot(mine, out_weight, preferred_element_type=jnp.float32)
    far_out = jnp.dot(mine, far_out_weight, preferred_element_type=jnp.float32)
    partial_out = jnp.concatenate(
        [jnp.where(first_core, near_out, far_out), jnp.where(first_core, far_out, near_out)], axis=1
    ).astype(jnp.bfloat16)
    per_batch = side * side // batches
    arrived = lax.all_to_all(
        partial_out.reshape(batches, per_batch * seq_count, -1),
        "batch",
        split_axis=0,
        concat_axis=0,
        tiled=True,
    )
    rows = stream.reshape(batches, per_batch, cores, seq_count, features_here)
    rows = lax.dynamic_index_in_dim(rows, batch_at, 0, keepdims=False)

    def of_core(core):
        taken = lax.dynamic_index_in_dim(rows, core, 1, keepdims=False).reshape(-1, features_here)
        return jnp.concatenate([taken.astype(jnp.float32), final_gain[None]], axis=0)

    near_rows = of_core(core_at)
    far_rows = shifted(of_core(1 - core_at), "mp_2", 1)
    both = jnp.concatenate(
        [jnp.where(first_core, near_rows, far_rows), jnp.where(first_core, far_rows, near_rows)],
        axis=1,
    )
    residual = both[:-1] + jnp.sum(arrived.astype(jnp.float32), axis=0)
    payload = (residual * both[-1:]).astype(jnp.bfloat16)
    gathered = sent_to_all(payload, BATCH_CORE).reshape(batches, cores, per_batch, seq_count, -1)
    scaled_out = jnp.moveaxis(gathered, 1, 2).reshape(seqs, -1)
    unscaled = scaled_out.astype(jnp.float32) / both[-1:]
    squares_here = jnp.sum(unscaled * unscaled, axis=1)
    squares_out = summed_along([squares_here] * side, "mp_0")
    near = jnp.where(first_core, scaled_out[:, :features_here], scaled_out[:, features_here:])
    far = jnp.where(first_core, scaled_out[:, features_here:], scaled_out[:, :features_here])
    upper, lower = head_partials(
        near, far, head_weight, far_head_weight, x_at, y_at, core_at, side, cores
    )
    squares_out = summed_along([squares_out] * side, "mp_1")
    scale_out = lax.rsqrt(squares_out / full_width + EPS)
    upper = summed_along(upper, "mp_0").astype(jnp.bfloat16)
    lower = summed_along(lower, "mp_1").astype(jnp.bfloat16)
    upper = summed_along([upper[k] for k in range(side)], "mp_1")
    lower = summed_along([lower[k] for k in range(side)], "mp_0")
    logits = jnp.concatenate([upper, lower], axis=0) * scale_out[:, None]

    local_top = jnp.max(logits, axis=1)
    local_sum = jnp.sum(jnp.exp(logits - local_top[:, None]), axis=1)
    highest, summed = joined_all(local_top, local_sum, (BATCH_MP,))
    return (logits, jnp.log(summed) + highest)


def solution(mesh):
    torus = Mesh(
        mesh.devices.reshape(mesh.shape["batch"], 4, 4, 2), ("batch", "mp_0", "mp_1", "mp_2")
    )
    in_specs = (
        P(None, MP),
        P(MP),
        P("batch"),
        P(MP, "batch"),
        P("batch", MP),
        P(None, "batch", MP, None, None),
        P(MP, None),
        P(MP),
        P(MP),
        P(MP, "batch"),
    )
    out_specs = (P(None, BATCH_MP), P())

    def step(*args):
        return local(*args)

    step = jax.shard_map(step, mesh=torus, in_specs=in_specs, out_specs=out_specs, check_vma=False)
    return step
```

profile of v0, /device:TPU:1, one launch (start us, length us, event | category | flops | bytes accessed | tf_op | source)
XLA Modules:
  0.0 167.1 jit_solution(1397407745896030814)
XLA Ops:
  0.7 1.1 fusion.15
  1.9 0.2 copy.49
  2.1 0.2 copy.48
  2.2 1.2 fusion.6
  3.5 1.0 concatenate.35
  4.5 8.6 %all-to-all-start = ((bf16[32,8,1152]{2,1,0:T(8,128)(2,1)}), bf16[32,8,1152]{2,1,0:T(8,128)(2,1)S(1)}, u32[]{:S(2)}, u32[]{:S(2)}) async-start(bf16[32,8,1152]{2,1,0:T(8,128)(2,1)} %concatenate.35), calls=%async_computation | async-start | bytes 1179648 | tf_op jit(solution)/shard_map/all_to_all | solution.py:222
  13.1 0.3 collective-permute-start.1
  13.4 0.3 collective-permute-start.2
  13.7 0.7 add_convert_fusion.3
  14.4 0.8 select_reduce_fusion
  15.2 0.8 fusion.38
  16.1 0.7 select_reduce_fusion.5
  17.0 8.3 %all-to-all-done = bf16[32,8,1152]{2,1,0:T(8,128)(2,1)S(1)} async-done(((bf16[32,8,1152]{2,1,0:T(8,128)(2,1)}), bf16[32,8,1152]{2,1,0:T(8,128)(2,1)S(1)}, u32[]{:S(2)}, u32[]{:S(2)}) %all-to-all-start) | async-done | bytes 589856 | tf_op jit(solution)/shard_map/all_to_all | solution.py:222
  25.3 0.2 fusion.31
  25.8 0.3 fusion.13
  26.1 2.8 %fusion.54 = (f32[64,8]{1,0:T(8,128)S(1)}, f32[64,8,128]{2,1,0:T(8,128)S(1)}) fusion(bf16[64,8,128]{2,1,0:T(8,128)(2,1)S(1)} %bitcast.101, bf16[2,1,64,128,128]{4,3,2,1,0:T(8,128)(2,1)} %param.15, pred[64,128]{1,0:T(8,128)(4,1)S(1)} %add_compare_fusion), kind=kOutput, calls=%fused_computation.121 | convolution fusion | flops 16973312 | bytes 2500608 | tf_op jit(solution)/shard_map/phgd,hprd->hpgr/dot_general | solution.py:94
  29.3 0.2 fusion.25
  29.9 2.3 %fusion = f32[64,8,128]{2,1,0:T(8,128)S(1)} fusion(bf16[2,1,64,128,128]{4,3,2,1,0:T(8,128)(2,1)} %param.15, f32[64,8,128]{2,1,0:T(8,128)S(1)} %get-tuple-element.48, f32[64,8]{1,0:T(8,128)S(1)} %copy.53, f32[64,8]{1,0:T(8,128)S(1)} %copy.51, pred[64,128]{1,0:T(8,128)(4,1)S(1)} %add_compare_fusion), kind=kOutput, calls=%fused_computation | convolution fusion | flops 17039360 | bytes 2633728 | tf_op jit(solution)/shard_map/hpgr,hprd->phgd/dot_general | solution.py:108
  32.2 0.2 convolution_convert_fusion.2
  32.4 0.7 broadcast_in_dim.183
  33.2 3.5 %all-to-all-start.1 = ((bf16[16,8,1024]{2,1,0:T(8,128)(2,1)}), bf16[16,8,1024]{2,1,0:T(8,128)(2,1)S(1)}, u32[]{:S(2)}, u32[]{:S(2)}) async-start(bf16[16,8,1024]{2,1,0:T(8,128)(2,1)} %broadcast_in_dim.183), calls=%async_computation.1 | async-start | bytes 524288 | tf_op jit(solution)/shard_map/all_to_all | solution.py:26
  36.7 0.7 bitcast_convert_fusion.1
  37.5 0.2 collective-permute-start
  37.6 7.0 %all-to-all-done.1 = bf16[16,8,1024]{2,1,0:T(8,128)(2,1)S(1)} async-done(((bf16[16,8,1024]{2,1,0:T(8,128)(2,1)}), bf16[16,8,1024]{2,1,0:T(8,128)(2,1)S(1)}, u32[]{:S(2)}, u32[]{:S(2)}) %all-to-all-start.1) | async-done | bytes 262176 | tf_op jit(solution)/shard_map/all_to_all | solution.py:26
  44.6 0.2 fusion.23
  44.9 0.2 select_convert_fusion.1
  45.1 0.7 pad_maximum_fusion
  45.8 8.2 %all-to-all-start.2 = ((bf16[8,16,512]{2,1,0:T(8,128)(2,1)}), bf16[8,16,512]{2,1,0:T(8,128)(2,1)S(1)}, u32[]{:S(2)}, u32[]{:S(2)}) async-start(bf16[8,16,512]{2,1,0:T(8,128)(2,1)} %pad_maximum_fusion), calls=%async_computation.2 | async-start | bytes 262144 | tf_op jit(solution)/shard_map/all_to_all | solution.py:238
  54.0 7.9 %all-to-all-done.2 = bf16[8,16,512]{2,1,0:T(8,128)(2,1)S(1)} async-done(((bf16[8,16,512]{2,1,0:T(8,128)(2,1)}), bf16[8,16,512]{2,1,0:T(8,128)(2,1)S(1)}, u32[]{:S(2)}, u32[]{:S(2)}) %all-to-all-start.2) | async-done | bytes 131104 | tf_op jit(solution)/shard_map/all_to_all | solution.py:238
  61.9 0.7 broadcast_in_dim.184
  62.7 6.3 %all-to-all-start.3 = ((bf16[16,16,512]{2,1,0:T(8,128)(2,1)}), bf16[16,16,512]{2,1,0:T(8,128)(2,1)S(1)}, u32[]{:S(2)}, u32[]{:S(2)}) async-start(bf16[16,16,512]{2,1,0:T(8,128)(2,1)} %broadcast_in_dim.184), calls=%async_computation.3 | async-start | bytes 524288 | tf_op jit(solution)/shard_map/all_to_all | solution.py:26
  68.9 0.7 pad_add_fusion.place
  69.6 11.1 %all-to-all-done.3 = bf16[16,16,512]{2,1,0:T(8,128)(2,1)S(1)} async-done(((bf16[16,16,512]{2,1,0:T(8,128)(2,1)}), bf16[16,16,512]{2,1,0:T(8,128)(2,1)S(1)}, u32[]{:S(2)}, u32[]{:S(2)}) %all-to-all-start.3) | async-done | bytes 262176 | tf_op jit(solution)/shard_map/all_to_all | solution.py:26
  80.7 0.2 multiply_reduce_fusion
  81.0 0.8 collective-permute-start.17
  81.8 1.0 collective-permute-start.16
  82.9 0.7 broadcast_select_fusion
  83.7 9.2 %head_partials.1 = (bf16[4,128,384]{2,1,0:T(8,128)(2,1)}, bf16[4,128,384]{2,1,0:T(8,128)(2,1)}, bf16[4,128,384]{2,1,0:T(8,128)(2,1)}, bf16[4,128,384]{2,1,0:T(8,...) custom-call(s32[3]{0:T(128)} %pad_add_fusion.place, ...), custom_call_target="tpu_custom_call" | custom-call | tf_op jit(solution)/shard_map/head_partials/pallas_call | solution.py:154
  92.9 1.6 collective-permute-start.3
  94.5 2.2 %collective-permute-start.4 = (bf16[4,128,384]{2,1,0:T(8,128)(2,1)}, bf16[4,128,384]{2,1,0:T(8,128)(2,1)S(1)}, u32[]{:S(2)}, u32[]{:S(2)}) collective-permute-start(bf16[4,128,384]{2,1,0:T(8,128)(2,1)} %get-tuple-element.12), channel_id=1, source_target_pairs={{0,16},{8,24},{16,0},{24,8},{1,17},{9,25},{17,1},{25,9},{2,18},{10... | collective-permute-start | bytes 1179656 | tf_op jit(solution)/shard_map/ppermute | solution.py:31
  96.7 1.5 collective-permute-start.5
  98.3 0.8 collective-permute-start.20
  99.1 1.3 collective-permute-start.19
  100.4 0.8 collective-permute-done.20
  101.4 1.7 collective-permute-done.19
  103.0 2.1 %collective-permute-done.18 = f32[256]{0:T(256)S(1)} collective-permute-done((f32[256]{0:T(256)S(1)}, f32[256]{0:T(256)S(1)}, u32[]{:S(2)}, u32[]{:S(2)}) %collective-permute-start.18) | collective-permute-done | bytes 1056 | tf_op jit(solution)/shard_map/ppermute | solution.py:31
  105.2 1.8 %collective-permute-start.10 = (bf16[4,128,384]{2,1,0:T(8,128)(2,1)}, bf16[4,128,384]{2,1,0:T(8,128)(2,1)S(1)}, u32[]{:S(2)}, u32[]{:S(2)}) collective-permute-start(bf16[4,128,384]{2,1,0:T(8,128)(2,1)} %get-tuple-element.16), channel_id=1, source_target_pairs={{0,4},{2,6},{4,0},{6,2},{1,5},{3,7},{5,1},{7,3},{8,12},{10,14},{12... | collective-permute-start | bytes 1179656 | tf_op jit(solution)/shard_map/ppermute | solution.py:31
  107.0 0.9 collective-permute-start.11
  107.9 6.4 %collective-permute-done.4 = bf16[4,128,384]{2,1,0:T(8,128)(2,1)S(1)} collective-permute-done((bf16[4,128,384]{2,1,0:T(8,128)(2,1)}, bf16[4,128,384]{2,1,0:T(8,128)(2,1)S(1)}, u32[]{:S(2)}, u32[]{:S(2)}) %collective-permute-start.4) | collective-permute-done | bytes 393248 | tf_op jit(solution)/shard_map/ppermute | solution.py:31
  114.3 1.2 add_convert_fusion.1
  115.6 2.7 %collective-permute-start.8 = (bf16[128,384]{1,0:T(8,128)(2,1)S(1)}, bf16[128,384]{1,0:T(8,128)(2,1)S(1)}, u32[]{:S(2)}, u32[]{:S(2)}) collective-permute-start(bf16[128,384]{1,0:T(8,128)(2,1)S(1)} %get-tuple-element.26), channel_id=1, source_target_pairs={{0,6},{2,0},{4,2},{6,4},{1,7},{3,1},{5,3},{7,5},{8,14},{10,8},{12,... | collective-permute-start | bytes 294920 | tf_op jit(solution)/shard_map/ppermute | solution.py:31
  118.3 0.1 collective-permute-start.7
  118.4 3.6 %collective-permute-done.10 = bf16[4,128,384]{2,1,0:T(8,128)(2,1)S(1)} collective-permute-done((bf16[4,128,384]{2,1,0:T(8,128)(2,1)}, bf16[4,128,384]{2,1,0:T(8,128)(2,1)S(1)}, u32[]{:S(2)}, u32[]{:S(2)}) %collective-permute-start.10) | collective-permute-done | bytes 393248 | tf_op jit(solution)/shard_map/ppermute | solution.py:31
  122.0 3.4 %collective-permute-done.11 = bf16[4,128,384]{2,1,0:T(8,128)(2,1)S(1)} collective-permute-done((bf16[4,128,384]{2,1,0:T(8,128)(2,1)}, bf16[4,128,384]{2,1,0:T(8,128)(2,1)S(1)}, u32[]{:S(2)}, u32[]{:S(2)}) %collective-permute-start.11) | collective-permute-done | bytes 393248 | tf_op jit(solution)/shard_map/ppermute | solution.py:31
  125.4 1.2 add_convert_fusion
  126.7 2.7 %collective-permute-start.14 = (bf16[128,384]{1,0:T(8,128)(2,1)S(1)}, bf16[128,384]{1,0:T(8,128)(2,1)S(1)}, u32[]{:S(2)}, u32[]{:S(2)}) collective-permute-start(bf16[128,384]{1,0:T(8,128)(2,1)S(1)} %get-tuple-element.29), channel_id=1, source_target_pairs={{0,24},{8,0},{16,8},{24,16},{1,25},{9,1},{17,9},{25,17},{2,26},{10... | collective-permute-start | bytes 294920 | tf_op jit(solution)/shard_map/ppermute | solution.py:31
  129.4 1.9 %collective-permute-done.12 = bf16[128,384]{1,0:T(8,128)(2,1)S(1)} collective-permute-done((bf16[128,384]{1,0:T(8,128)(2,1)S(1)}, bf16[128,384]{1,0:T(8,128)(2,1)S(1)}, u32[]{:S(2)}, u32[]{:S(2)}) %collective-permute-start.12) | collective-permute-done | bytes 98336 | tf_op jit(solution)/shard_map/ppermute | solution.py:31
  131.4 0.6 collective-permute-done.14
  132.0 3.5 %collective-permute-done.13 = bf16[128,384]{1,0:T(8,128)(2,1)S(1)} collective-permute-done((bf16[128,384]{1,0:T(8,128)(2,1)S(1)}, bf16[128,384]{1,0:T(8,128)(2,1)S(1)}, u32[]{:S(2)}, u32[]{:S(2)}) %collective-permute-start.13) | collective-permute-done | bytes 98336 | tf_op jit(solution)/shard_map/ppermute | solution.py:31
  135.5 0.2 fusion.52
  135.7 0.2 exponential_reduce_fusion
  136.0 29.9 %all_to_all.25 = f32[256,2,256]{2,1,0:T(2,128)S(1)} all-to-all(f32[256,2,256]{2,1,0:T(2,128)S(1)} %broadcast_in_dim.185), channel_id=1, replica_groups=mesh['batch'=8,'mp_0'=4,'mp_1'=4,'mp_2'=2] {'batch','mp_0','mp_1','mp_2'}, dimensions={0} | all-to-all | bytes 1048576 | tf_op jit(solution)/shard_map/all_to_all | solution.py:26
  165.9 0.5 fusion.53
  166.5 0.6 log_add_fusion
  (69 shorter events, 2.5 us)
Async XLA Ops:
  0.6 1.6 copy-start
  0.6 25.0 %copy-start.3 = (f32[1024]{0:T(1024)S(1)}, f32[1024]{0:T(1024)}, u32[]{:S(2)}) copy-start(f32[1024]{0:T(1024)} %param.12) | copy-start | bytes 12292
  4.5 20.8 %all-to-all-start = ((bf16[32,8,1152]{2,1,0:T(8,128)(2,1)}), bf16[32,8,1152]{2,1,0:T(8,128)(2,1)S(1)}, u32[]{:S(2)}, u32[]{:S(2)}) async-start(bf16[32,8,1152]{2,1,0:T(8,128)(2,1)} %concatenate.35), calls=%async_computation | async-start | bytes 1179648 | tf_op jit(solution)/shard_map/all_to_all | solution.py:222
  13.1 31.8 %collective-permute-start.1 = (bf16[1024,256]{1,0:T(8,128)(2,1)}, bf16[1024,256]{1,0:T(8,128)(2,1)S(1)}, u32[]{:S(2)}, u32[]{:S(2)}) collective-permute-start(bf16[1024,256]{1,0:T(8,128)(2,1)} %param.14), channel_id=1, source_target_pairs={{0,1},{1,0},{2,3},{3,2},{4,5},{5,4},{6,7},{7,6},{8,9},{9,8},{10,11... | collective-permute-start | bytes 1572872 | tf_op jit(solution)/shard_map/ppermute | solution.py:31
  13.4 70.3 %collective-permute-start.2 = (bf16[256,12288]{1,0:T(8,128)(2,1)}, bf16[256,12288]{1,0:T(8,128)(2,1)}, u32[]{:S(2)}, u32[]{:S(2)}) collective-permute-start(bf16[256,12288]{1,0:T(8,128)(2,1)} %refs_3_.1), channel_id=1, source_target_pairs={{0,1},{1,0},{2,3},{3,2},{4,5},{5,4},{6,7},{7,6},{8,9},{9,8},{10,11... | collective-permute-start | bytes 18874376 | tf_op jit(solution)/shard_map/ppermute | solution.py:31
  25.6 11.8 %copy-start.4 = (f32[256]{0:T(256)S(1)}, f32[256]{0:T(256)}, u32[]{:S(2)}) copy-start(f32[256]{0:T(256)} %param.18) | copy-start | bytes 3076
  25.6 19.0 %copy-start.2 = (bf16[1024,256]{1,0:T(8,128)(2,1)S(1)}, bf16[1024,256]{1,0:T(8,128)(2,1)}, u32[]{:S(2)}) copy-start(bf16[1024,256]{1,0:T(8,128)(2,1)} %param.14) | copy-start | bytes 1572868
  33.2 11.4 %all-to-all-start.1 = ((bf16[16,8,1024]{2,1,0:T(8,128)(2,1)}), bf16[16,8,1024]{2,1,0:T(8,128)(2,1)S(1)}, u32[]{:S(2)}, u32[]{:S(2)}) async-start(bf16[16,8,1024]{2,1,0:T(8,128)(2,1)} %broadcast_in_dim.183), calls=%async_computation.1 | async-start | bytes 524288 | tf_op jit(solution)/shard_map/all_to_all | solution.py:26
  37.5 16.5 %collective-permute-start = (f32[17,256]{1,0:T(8,128)S(1)}, f32[17,256]{1,0:T(8,128)S(1)}, u32[]{:S(2)}, u32[]{:S(2)}) collective-permute-start(f32[17,256]{1,0:T(8,128)S(1)} %pad_maximum_fusion.1), channel_id=1, source_target_pairs={{0,1},{1,0},{2,3},{3,2},{4,5},{5,4},{6,7},{7,6},{8,9},{9,8},{10,11... | collective-permute-start | bytes 52232 | tf_op jit(solution)/shard_map/ppermute | solution.py:31
  45.8 16.1 %all-to-all-start.2 = ((bf16[8,16,512]{2,1,0:T(8,128)(2,1)}), bf16[8,16,512]{2,1,0:T(8,128)(2,1)S(1)}, u32[]{:S(2)}, u32[]{:S(2)}) async-start(bf16[8,16,512]{2,1,0:T(8,128)(2,1)} %pad_maximum_fusion), calls=%async_computation.2 | async-start | bytes 262144 | tf_op jit(solution)/shard_map/all_to_all | solution.py:238
  62.7 18.0 %all-to-all-start.3 = ((bf16[16,16,512]{2,1,0:T(8,128)(2,1)}), bf16[16,16,512]{2,1,0:T(8,128)(2,1)S(1)}, u32[]{:S(2)}, u32[]{:S(2)}) async-start(bf16[16,16,512]{2,1,0:T(8,128)(2,1)} %broadcast_in_dim.184), calls=%async_computation.3 | async-start | bytes 524288 | tf_op jit(solution)/shard_map/all_to_all | solution.py:26
  81.0 15.8 %collective-permute-start.17 = (f32[256]{0:T(256)S(1)}, f32[256]{0:T(256)S(1)}, u32[]{:S(2)}, u32[]{:S(2)}) collective-permute-start(f32[256]{0:T(256)S(1)} %reduce_sum.136), channel_id=1, source_target_pairs={{0,24},{8,0},{16,8},{24,16},{1,25},{9,1},{17,9},{25,17},{2,26},{10... | collective-permute-start | bytes 3080 | tf_op jit(solution)/shard_map/ppermute | solution.py:31
  81.8 16.4 %collective-permute-start.16 = (f32[256]{0:T(256)S(1)}, f32[256]{0:T(256)S(1)}, u32[]{:S(2)}, u32[]{:S(2)}) collective-permute-start(f32[256]{0:T(256)S(1)} %reduce_sum.136), channel_id=1, source_target_pairs={{0,16},{8,24},{16,0},{24,8},{1,17},{9,25},{17,1},{25,9},{2,18},{10... | collective-permute-start | bytes 3080 | tf_op jit(solution)/shard_map/ppermute | solution.py:31
  82.8 15.4 %collective-permute-start.15 = (f32[256]{0:T(256)S(1)}, f32[256]{0:T(256)S(1)}, u32[]{:S(2)}, u32[]{:S(2)}) collective-permute-start(f32[256]{0:T(256)S(1)} %reduce_sum.136), channel_id=1, source_target_pairs={{0,8},{8,16},{16,24},{24,0},{1,9},{9,17},{17,25},{25,1},{2,10},{10... | collective-permute-start | bytes 3080 | tf_op jit(solution)/shard_map/ppermute | solution.py:31
  92.9 14.0 %collective-permute-start.3 = (bf16[4,128,384]{2,1,0:T(8,128)(2,1)}, bf16[4,128,384]{2,1,0:T(8,128)(2,1)S(1)}, u32[]{:S(2)}, u32[]{:S(2)}) collective-permute-start(bf16[4,128,384]{2,1,0:T(8,128)(2,1)} %get-tuple-element.11), channel_id=1, source_target_pairs={{0,8},{8,16},{16,24},{24,0},{1,9},{9,17},{17,25},{25,1},{2,10},{10... | collective-permute-start | bytes 1179656 | tf_op jit(solution)/shard_map/ppermute | solution.py:31
  94.5 19.8 %collective-permute-start.4 = (bf16[4,128,384]{2,1,0:T(8,128)(2,1)}, bf16[4,128,384]{2,1,0:T(8,128)(2,1)S(1)}, u32[]{:S(2)}, u32[]{:S(2)}) collective-permute-start(bf16[4,128,384]{2,1,0:T(8,128)(2,1)} %get-tuple-element.12), channel_id=1, source_target_pairs={{0,16},{8,24},{16,0},{24,8},{1,17},{9,25},{17,1},{25,9},{2,18},{10... | collective-permute-start | bytes 1179656 | tf_op jit(solution)/shard_map/ppermute | solution.py:31
  96.7 17.6 %collective-permute-start.5 = (bf16[4,128,384]{2,1,0:T(8,128)(2,1)}, bf16[4,128,384]{2,1,0:T(8,128)(2,1)S(1)}, u32[]{:S(2)}, u32[]{:S(2)}) collective-permute-start(bf16[4,128,384]{2,1,0:T(8,128)(2,1)} %get-tuple-element.13), channel_id=1, source_target_pairs={{0,24},{8,0},{16,8},{24,16},{1,25},{9,1},{17,9},{25,17},{2,26},{10... | collective-permute-start | bytes 1179656 | tf_op jit(solution)/shard_map/ppermute | solution.py:31
  98.3 3.0 %collective-permute-start.20 = (f32[256]{0:T(256)S(1)}, f32[256]{0:T(256)S(1)}, u32[]{:S(2)}, u32[]{:S(2)}) collective-permute-start(f32[256]{0:T(256)S(1)} %add_add_fusion), channel_id=1, source_target_pairs={{0,6},{2,0},{4,2},{6,4},{1,7},{3,1},{5,3},{7,5},{8,14},{10,8},{12,... | collective-permute-start | bytes 3080 | tf_op jit(solution)/shard_map/ppermute | solution.py:31
  99.1 3.9 %collective-permute-start.19 = (f32[256]{0:T(256)S(1)}, f32[256]{0:T(256)S(1)}, u32[]{:S(2)}, u32[]{:S(2)}) collective-permute-start(f32[256]{0:T(256)S(1)} %add_add_fusion), channel_id=1, source_target_pairs={{0,4},{2,6},{4,0},{6,2},{1,5},{3,7},{5,1},{7,3},{8,12},{10,14},{12... | collective-permute-start | bytes 3080 | tf_op jit(solution)/shard_map/ppermute | solution.py:31
  101.2 3.9 %collective-permute-start.18 = (f32[256]{0:T(256)S(1)}, f32[256]{0:T(256)S(1)}, u32[]{:S(2)}, u32[]{:S(2)}) collective-permute-start(f32[256]{0:T(256)S(1)} %add_add_fusion), channel_id=1, source_target_pairs={{0,2},{2,4},{4,6},{6,0},{1,3},{3,5},{5,7},{7,1},{8,10},{10,12},{12... | collective-permute-start | bytes 3080 | tf_op jit(solution)/shard_map/ppermute | solution.py:31
  105.2 13.1 %collective-permute-start.9 = (bf16[4,128,384]{2,1,0:T(8,128)(2,1)}, bf16[4,128,384]{2,1,0:T(8,128)(2,1)S(1)}, u32[]{:S(2)}, u32[]{:S(2)}) collective-permute-start(bf16[4,128,384]{2,1,0:T(8,128)(2,1)} %get-tuple-element.15), channel_id=1, source_target_pairs={{0,2},{2,4},{4,6},{6,0},{1,3},{3,5},{5,7},{7,1},{8,10},{10,12},{12... | collective-permute-start | bytes 1179656 | tf_op jit(solution)/shard_map/ppermute | solution.py:31
  105.2 16.8 %collective-permute-start.10 = (bf16[4,128,384]{2,1,0:T(8,128)(2,1)}, bf16[4,128,384]{2,1,0:T(8,128)(2,1)S(1)}, u32[]{:S(2)}, u32[]{:S(2)}) collective-permute-start(bf16[4,128,384]{2,1,0:T(8,128)(2,1)} %get-tuple-element.16), channel_id=1, source_target_pairs={{0,4},{2,6},{4,0},{6,2},{1,5},{3,7},{5,1},{7,3},{8,12},{10,14},{12... | collective-permute-start | bytes 1179656 | tf_op jit(solution)/shard_map/ppermute | solution.py:31
  107.0 18.4 %collective-permute-start.11 = (bf16[4,128,384]{2,1,0:T(8,128)(2,1)}, bf16[4,128,384]{2,1,0:T(8,128)(2,1)S(1)}, u32[]{:S(2)}, u32[]{:S(2)}) collective-permute-start(bf16[4,128,384]{2,1,0:T(8,128)(2,1)} %get-tuple-element.17), channel_id=1, source_target_pairs={{0,6},{2,0},{4,2},{6,4},{1,7},{3,1},{5,3},{7,5},{8,14},{10,8},{12,... | collective-permute-start | bytes 1179656 | tf_op jit(solution)/shard_map/ppermute | solution.py:31
  115.5 13.8 %collective-permute-start.6 = (bf16[128,384]{1,0:T(8,128)(2,1)S(1)}, bf16[128,384]{1,0:T(8,128)(2,1)S(1)}, u32[]{:S(2)}, u32[]{:S(2)}) collective-permute-start(bf16[128,384]{1,0:T(8,128)(2,1)S(1)} %get-tuple-element.25), channel_id=1, source_target_pairs={{0,2},{2,4},{4,6},{6,0},{1,3},{3,5},{5,7},{7,1},{8,10},{10,12},{12... | collective-permute-start | bytes 294920 | tf_op jit(solution)/shard_map/ppermute | solution.py:31
  115.6 13.7 %collective-permute-start.8 = (bf16[128,384]{1,0:T(8,128)(2,1)S(1)}, bf16[128,384]{1,0:T(8,128)(2,1)S(1)}, u32[]{:S(2)}, u32[]{:S(2)}) collective-permute-start(bf16[128,384]{1,0:T(8,128)(2,1)S(1)} %get-tuple-element.26), channel_id=1, source_target_pairs={{0,6},{2,0},{4,2},{6,4},{1,7},{3,1},{5,3},{7,5},{8,14},{10,8},{12,... | collective-permute-start | bytes 294920 | tf_op jit(solution)/shard_map/ppermute | solution.py:31
  118.3 11.1 %collective-permute-start.7 = (bf16[128,384]{1,0:T(8,128)(2,1)S(1)}, bf16[128,384]{1,0:T(8,128)(2,1)S(1)}, u32[]{:S(2)}, u32[]{:S(2)}) collective-permute-start(bf16[128,384]{1,0:T(8,128)(2,1)S(1)} %get-tuple-element.27), channel_id=1, source_target_pairs={{0,4},{2,6},{4,0},{6,2},{1,5},{3,7},{5,1},{7,3},{8,12},{10,14},{12... | collective-permute-start | bytes 294920 | tf_op jit(solution)/shard_map/ppermute | solution.py:31
  126.6 4.8 %collective-permute-start.12 = (bf16[128,384]{1,0:T(8,128)(2,1)S(1)}, bf16[128,384]{1,0:T(8,128)(2,1)S(1)}, u32[]{:S(2)}, u32[]{:S(2)}) collective-permute-start(bf16[128,384]{1,0:T(8,128)(2,1)S(1)} %get-tuple-element.28), channel_id=1, source_target_pairs={{0,8},{8,16},{16,24},{24,0},{1,9},{9,17},{17,25},{25,1},{2,10},{10... | collective-permute-start | bytes 294920 | tf_op jit(solution)/shard_map/ppermute | solution.py:31
  126.7 5.3 %collective-permute-start.14 = (bf16[128,384]{1,0:T(8,128)(2,1)S(1)}, bf16[128,384]{1,0:T(8,128)(2,1)S(1)}, u32[]{:S(2)}, u32[]{:S(2)}) collective-permute-start(bf16[128,384]{1,0:T(8,128)(2,1)S(1)} %get-tuple-element.29), channel_id=1, source_target_pairs={{0,24},{8,0},{16,8},{24,16},{1,25},{9,1},{17,9},{25,17},{2,26},{10... | collective-permute-start | bytes 294920 | tf_op jit(solution)/shard_map/ppermute | solution.py:31
  129.4 6.1 %collective-permute-start.13 = (bf16[128,384]{1,0:T(8,128)(2,1)S(1)}, bf16[128,384]{1,0:T(8,128)(2,1)S(1)}, u32[]{:S(2)}, u32[]{:S(2)}) collective-permute-start(bf16[128,384]{1,0:T(8,128)(2,1)S(1)} %get-tuple-element.30), channel_id=1, source_target_pairs={{0,16},{8,24},{16,0},{24,8},{1,17},{9,25},{17,1},{25,9},{2,18},{10... | collective-permute-start | bytes 294920 | tf_op jit(solution)/shard_map/ppermute | solution.py:31
  135.7 31.5 %copy-start.1 = (f32[256,384]{1,0:T(8,128)}, f32[256,384]{1,0:T(8,128)S(1)}, u32[]{:S(2)}) copy-start(f32[256,384]{1,0:T(8,128)S(1)} %get-tuple-element.21) | copy-start | bytes 1179652
where the time goes:
time: 168 us; the launch traced here: 167 us
  waiting for transfers between devices  58.2 us (35%)
  starting transfers between devices  45.2 us (27%)
  blocking collectives  29.9 us (18%)
  other arithmetic  12.6 us (8%)
  Pallas kernels  9.25 us (6%)
  matrix products  7.31 us (4%)
  local copies, waits for them, and re-layouts  3.62 us (2%)
    all_to_all x1, blocking collectives, sent_to_all(): lax.all_to_all(jnp.broadcast_to(x[None], (length, *x.shape)), axis, 0, 0,...  29.9 us
    ppermute x21, waiting for transfers between devices, shifted(): lax.ppermute(x, axis, [(k, (k + by) % length) for k in range(length)])  24 us
    ppermute x21, starting transfers between devices, shifted(): lax.ppermute(x, axis, [(k, (k + by) % length) for k in range(length)])  18.7 us
    all_to_all x2, waiting for transfers between devices, sent_to_all(): lax.all_to_all(jnp.broadcast_to(x[None], (length, *x.shape)), axis, 0, 0,...  18.1 us
    all_to_all x2, starting transfers between devices, sent_to_all(): lax.all_to_all(jnp.broadcast_to(x[None], (length, *x.shape)), axis, 0, 0,...  9.8 us
    pallas_call x1, Pallas kernels, head_partials(): pl.pallas_call(head_block, grid_spec=pltpu.PrefetchScalarGridSpec(num_sca...  9.25 us
    all_to_all x1, starting transfers between devices, local(): lax.all_to_all(payload.reshape(members, seq_count, -1), MP, split_axis=0,...  8.58 us
    all_to_all x1, waiting for transfers between devices, local(): lax.all_to_all(payload.reshape(members, seq_count, -1), MP, split_axis=0,...  8.31 us
  transfers between devices with their start and end apart: 25, of which 13 were waited for; matrix products, arithmetic and copies ran while one was open for 11% of the time, Pallas kernels for 6%

commit v1 on v0

v1 whole, which is shorter than its diff:
```python
import functools
import math

import jax
import jax.numpy as jnp
from jax import lax
from jax.experimental import pallas as pl
from jax.experimental.pallas import tpu as pltpu
from jax.sharding import Mesh
from jax.sharding import PartitionSpec as P

MP = ("mp_0", "mp_1", "mp_2")
BATCH_MP = ("batch", "mp_0", "mp_1", "mp_2")
XY = ("mp_0", "mp_1")
BATCH_CORE = ("batch", "mp_2")


EPS = 1e-06
ROPE_BASE = 1000000.0
INTERPRET = False

LANES = 128


def sent_to_all(x, axis):
    length = lax.axis_size(axis)
    return lax.all_to_all(jnp.broadcast_to(x[None], (length, *x.shape)), axis, 0, 0, tiled=True)


def shifted(x, axis, by):
    length = lax.axis_size(axis)
    return lax.ppermute(x, axis, [(k, (k + by) % length) for k in range(length)])


def query_block(stream, gain, weight, out):
    width = weight.shape[1]
    features = stream[...].astype(jnp.float32)
    squares = jnp.sum(features * features, axis=1, keepdims=True)
    products = jnp.dot(
        (features * gain[...]).astype(jnp.bfloat16), weight[...], preferred_element_type=jnp.float32
    )
    out[:, :width] = products.astype(jnp.bfloat16)
    coarse = squares.astype(jnp.bfloat16).astype(jnp.float32)
    lane = lax.broadcasted_iota(jnp.int32, (features.shape[0], LANES), 1)
    tail = jnp.where(lane == 0, coarse, jnp.where(lane == 1, squares - coarse, 0.0))
    out[:, width:] = tail.astype(jnp.bfloat16)


def query_parts(stream, gain, weight):
    return pl.pallas_call(
        query_block,
        out_shape=jax.ShapeDtypeStruct((stream.shape[0], weight.shape[1] + LANES), jnp.bfloat16),
        interpret=INTERPRET,
        name="query_parts",
    )(stream, gain[None], weight)


def turns(position, head_size):
    half_dim = head_size // 2
    exponent = jnp.arange(half_dim, dtype=jnp.float32) * (-2.0 / head_size)
    frequency = ROPE_BASE**exponent
    angles = position.astype(jnp.float32)[:, None] * frequency[None, :]
    cosines, sines = jnp.cos(angles), jnp.sin(angles)
    return (
        jnp.concatenate([cosines, cosines], axis=1),
        jnp.concatenate([-sines, sines], axis=1),
    )


def token_owners(page_table, lengths, pool_size, page_size):
    seq_count, max_pages = page_table.shape
    page_order = jnp.arange(max_pages, dtype=jnp.int32)
    used_pages = (lengths + page_size - 1) // page_size
    slot_ids = jnp.arange(pool_size, dtype=jnp.int32)
    matches = (page_table[:, :, None] == slot_ids[None, None, :]) & (
        page_order[None, :, None] < used_pages[:, None, None]
    )
    seq_ids = jnp.arange(seq_count, dtype=jnp.int32)
    owner = jnp.sum(jnp.where(matches, seq_ids[:, None, None], 0), axis=(0, 1))
    remaining = lengths[:, None] - page_order[None, :] * page_size
    visible = jnp.sum(jnp.where(matches, remaining[:, :, None], 0), axis=(0, 1))
    at = jnp.arange(page_size, dtype=jnp.int32)
    return jnp.where(at[None, :] < visible[:, None], owner[:, None], -1)


def attend_block(full_width, sums, bias, cosines, sines, owners, pages, out, *scratch):
    keys, values, scores, sems = scratch
    copies, seq_count, width = out.shape
    pool_size, page_size, head_size = keys.shape
    heads = width // head_size
    rows = heads * seq_count
    chunks = sems.shape[1]
    slots = pool_size // chunks
    tokens = slots * page_size

    fetches = []
    for kind, held in enumerate((keys, values)):
        for k in range(chunks):
            at = pl.ds(k * slots, slots)
            copy = pltpu.make_async_copy(pages.at[kind, 0, at], held.at[at], sems.at[kind, k])
            copy.start()
            fetches.append(copy)

    tail = sums[:, width:]
    lane = lax.broadcasted_iota(jnp.int32, tail.shape, 1)
    squares = jnp.sum(jnp.where(lane < 2, tail, 0.0), axis=1, keepdims=True)
    turned = sums[:, :width] * lax.rsqrt(squares / full_width + EPS) + bias[...]
    pieces = []
    for k in range(heads):
        piece = turned[:, k * head_size : (k + 1) * head_size]
        across = pltpu.roll(piece, head_size // 2, 1)
        pieces.append(piece * cosines[...] + across * sines[...])
    queries = jnp.concatenate(pieces, axis=0).astype(jnp.bfloat16)

    row_seq = lax.broadcasted_iota(jnp.int32, (rows, 1), 0) % seq_count
    highest = jnp.full((rows, head_size), -1e30, jnp.float32)
    for k in range(chunks):
        fetches[k].wait()
        key = keys[k * slots : (k + 1) * slots].reshape(tokens, head_size)
        here = lax.dot_general(
            queries, key, (((1,), (1,)), ((), ())), preferred_element_type=jnp.float32
        ) * (1.0 / math.sqrt(head_size))
        at = slice(k * tokens, (k + 1) * tokens)
        here = jnp.where(owners[:, at] == row_seq, here, -1e30)
        scores[:, at] = here
        for t in range(tokens // head_size):
            highest = jnp.maximum(highest, here[:, t * head_size : (t + 1) * head_size])
    highest = jnp.max(highest, axis=1, keepdims=True)
    summed = jnp.zeros((rows, head_size), jnp.float32)
    mixed = jnp.zeros((rows, head_size), jnp.float32)
    for k in range(chunks):
        powers = jnp.exp(scores[:, k * tokens : (k + 1) * tokens] - highest)
        for t in range(tokens // head_size):
            summed += powers[:, t * head_size : (t + 1) * head_size]
        fetches[chunks + k].wait()
        value = values[k * slots : (k + 1) * slots].reshape(tokens, head_size)
        mixed += jnp.dot(powers.astype(jnp.bfloat16), value, preferred_element_type=jnp.float32)
    result = mixed / jnp.sum(summed, axis=1, keepdims=True)
    row = [result[k * seq_count : (k + 1) * seq_count] for k in range(heads)]
    row = jnp.concatenate(row, axis=1).astype(jnp.bfloat16)
    for k in range(copies):
        out[k] = row


def attend(sums, bias, cosines, sines, owners, page_cache, full_width, copies, chunks=8):
    seq_count, width = sums.shape
    width -= LANES
    pool_size, page_size, head_size = page_cache.shape[2:]
    pool = (pool_size, page_size, head_size)
    rows = width // head_size * seq_count
    in_hbm = pl.BlockSpec(memory_space=pltpu.HBM)
    in_vmem = pl.BlockSpec(memory_space=pltpu.VMEM)
    return pl.pallas_call(
        functools.partial(attend_block, full_width),
        in_specs=[in_vmem, in_vmem, in_vmem, in_vmem, in_vmem, in_hbm],
        out_specs=in_vmem,
        out_shape=jax.ShapeDtypeStruct((copies, seq_count, width), jnp.bfloat16),
        scratch_shapes=[
            pltpu.VMEM(pool, jnp.bfloat16),
            pltpu.VMEM(pool, jnp.bfloat16),
            pltpu.VMEM((rows, pool_size * page_size), jnp.float32),
            pltpu.SemaphoreType.DMA((2, chunks)),
        ],
        interpret=INTERPRET,
        name="attend",
    )(sums, bias[None], cosines, sines, owners.reshape(1, -1), page_cache)


def head_block(place, gain, gathered_far, near_weight, far_weight, *refs):
    batches, cores, per_batch, _, depth = gathered_far.shape
    side = (len(refs) - 7) // 2
    out_x, out_y = refs[:side], refs[side : 2 * side]
    gathered, weights, block_x, block_y, sem, sems_in, sems_out = refs[2 * side :]
    fetch = pltpu.make_async_copy(gathered_far, gathered, sem)
    fetch.start()
    x_at, y_at, core_at = place[0], place[1], place[2]
    width = near_weight.shape[1] // (side * side * cores)
    rows_here = depth // cores

    def weight_copies(x_to, y_to):
        column = (((x_at + x_to) % side) * side + (y_at + y_to) % side) * cores + core_at
        column = pl.multiple_of(column * width, width)
        copies = []
        for k, (weight, core) in enumerate(((near_weight, core_at), (far_weight, 1 - core_at))):
            row = pl.multiple_of(core * rows_here, rows_here)
            copies.append(
                pltpu.make_async_copy(
                    weight.at[:, pl.ds(column, width)],
                    weights.at[x_to, pl.ds(row, rows_here), pl.ds(y_to * width, width)],
                    sems_in.at[x_to, y_to * 2 + k],
                )
            )
        return copies

    loads = [[c for y_to in range(side) for c in weight_copies(x_to, y_to)] for x_to in range(side)]
    for copies in loads:
        for copy in copies:
            copy.start()

    fetch.wait()
    pieces = [
        gathered[b, c, i].astype(jnp.float32)
        for b in range(batches)
        for i in range(per_batch)
        for c in range(cores)
    ]
    ordered = jnp.concatenate(pieces, axis=0)
    features = ordered.astype(jnp.bfloat16)
    half = ordered.shape[0] // 2
    unscaled = ordered / gain[...]
    extra = block_x.shape[2] - half
    squares = lax.dot_general(
        jnp.ones((extra, depth), jnp.float32),
        unscaled * unscaled,
        (((1,), (1,)), ((), ())),
        precision=lax.Precision.HIGHEST,
        preferred_element_type=jnp.float32,
    )
    coarse = squares.astype(jnp.bfloat16)
    fine = (squares - coarse.astype(jnp.float32)).astype(jnp.bfloat16)
    filler = jnp.zeros((extra, width - 2 * half), jnp.bfloat16)
    tail_x = jnp.concatenate([coarse[:, :half], fine[:, :half], filler], axis=1)
    tail_y = jnp.concatenate([coarse[:, half:], fine[:, half:], filler], axis=1)

    stores = []
    for x_to in range(side):
        for copy in loads[x_to]:
            copy.wait()
        product = jnp.dot(features, weights[x_to], preferred_element_type=jnp.float32)
        for y_to in range(side):
            part = product[:, y_to * width : (y_to + 1) * width].astype(jnp.bfloat16)
            block_x[x_to, y_to, :half] = part[:half]
            block_x[x_to, y_to, half:] = tail_x
            block_y[y_to, x_to, :half] = part[half:]
            block_y[y_to, x_to, half:] = tail_y
            for copy in (
                pltpu.make_async_copy(
                    block_x.at[x_to, y_to], out_x[x_to].at[y_to], sems_out.at[0, x_to, y_to]
                ),
                pltpu.make_async_copy(
                    block_y.at[y_to, x_to], out_y[y_to].at[x_to], sems_out.at[1, x_to, y_to]
                ),
            ):
                copy.start()
                stores.append(copy)
    for copy in stores:
        copy.wait()


def head_partials(gathered, gain, near_weight, far_weight, x_at, y_at, core_at, side):
    batches, cores, per_batch, seq_count, depth = gathered.shape
    half = batches * cores * per_batch * seq_count // 2
    width = near_weight.shape[1] // (side * side * cores)
    block = (side, half + 8, width)
    in_hbm = pl.BlockSpec(memory_space=pltpu.HBM)
    outs = pl.pallas_call(
        head_block,
        in_specs=[
            pl.BlockSpec(memory_space=pltpu.SMEM),
            pl.BlockSpec(memory_space=pltpu.VMEM),
            in_hbm,
            in_hbm,
            in_hbm,
        ],
        out_specs=[in_hbm] * (2 * side),
        out_shape=[jax.ShapeDtypeStruct(block, jnp.bfloat16)] * (2 * side),
        scratch_shapes=[
            pltpu.VMEM(gathered.shape, jnp.bfloat16),
            pltpu.VMEM((side, depth, side * width), jnp.bfloat16),
            pltpu.VMEM((side, *block), jnp.bfloat16),
            pltpu.VMEM((side, *block), jnp.bfloat16),
            pltpu.SemaphoreType.DMA,
            pltpu.SemaphoreType.DMA((side, 2 * side)),
            pltpu.SemaphoreType.DMA((2, side, side)),
        ],
        interpret=INTERPRET,
        name="head_partials",
    )(
        jnp.stack([x_at, y_at, core_at]).astype(jnp.int32),
        gain,
        gathered,
        near_weight,
        far_weight,
    )
    return outs[:side], outs[side:]


def summed_along(parts, axis):
    arrived = [shifted(parts[k], axis, k) for k in range(1, len(parts))]
    total = parts[0].astype(jnp.float32)
    for piece in arrived:
        total = total + piece.astype(jnp.float32)
    return total


def joined_all(top, total, axes):
    for axis in axes:
        pieces = sent_to_all(jnp.stack([top, total]), axis)
        tops = pieces[:, 0]
        top = jnp.max(tops, axis=0)
        total = jnp.sum(pieces[:, 1] * jnp.exp(tops - top[None]), axis=0)
    return top, total


def local(
    stream,
    input_gain,
    query_bias,
    query_weight,
    out_weight,
    page_cache,
    page_table,
    lengths,
    final_gain,
    head_weight,
):
    side, cores, batches = lax.axis_size("mp_0"), lax.axis_size("mp_2"), lax.axis_size("batch")
    members = side * side * cores
    x_at, y_at, core_at = lax.axis_index("mp_0"), lax.axis_index("mp_1"), lax.axis_index("mp_2")
    batch_at = lax.axis_index("batch")
    first_core = core_at == 0
    seqs, features_here = stream.shape
    full_width = features_here * members
    seq_count = page_table.shape[0]
    head_size = page_cache.shape[-1]

    far_head_weight = shifted(head_weight, "mp_2", 1)
    far_out_weight = shifted(out_weight, "mp_2", 1)

    parts = query_parts(stream, input_gain, query_weight).reshape(members, seq_count, -1)
    parts = lax.all_to_all(parts, MP, split_axis=0, concat_axis=0, tiled=True)
    owners = token_owners(page_table, lengths, *page_cache.shape[2:4])
    cosines, sines = turns(lengths - 1, head_size)
    sums = jnp.sum(parts.astype(jnp.float32), axis=0)
    attended = attend(
        sums, query_bias, cosines, sines, owners, page_cache, full_width, side * side
    )

    mine = lax.all_to_all(attended, XY, 0, 0, tiled=True).reshape(side * side * seq_count, -1)
    both_out = jnp.concatenate(
        [
            jnp.where(first_core, out_weight, far_out_weight),
            jnp.where(first_core, far_out_weight, out_weight),
        ],
        axis=1,
    )
    both_out = lax.optimization_barrier(both_out)
    partial_out = jnp.dot(mine, both_out, preferred_element_type=jnp.float32).astype(jnp.bfloat16)
    per_batch = side * side // batches
    arrived = lax.all_to_all(
        partial_out.reshape(batches, per_batch * seq_count, -1),
        "batch",
        split_axis=0,
        concat_axis=0,
        tiled=True,
    )
    rows = stream.reshape(batches, per_batch, cores, seq_count, features_here)
    rows = lax.dynamic_index_in_dim(rows, batch_at, 0, keepdims=False)

    def of_core(core):
        taken = lax.dynamic_index_in_dim(rows, core, 1, keepdims=False).reshape(-1, features_here)
        return jnp.concatenate([taken.astype(jnp.float32), final_gain[None]], axis=0)

    near_rows = of_core(core_at)
    far_rows = shifted(of_core(1 - core_at), "mp_2", 1)
    both = jnp.concatenate(
        [jnp.where(first_core, near_rows, far_rows), jnp.where(first_core, far_rows, near_rows)],
        axis=1,
    )
    residual = both[:-1] + jnp.sum(arrived.astype(jnp.float32), axis=0)
    payload = (residual * both[-1:]).astype(jnp.bfloat16)
    gathered = sent_to_all(payload, BATCH_CORE).reshape(batches, cores, per_batch, seq_count, -1)
    upper, lower = head_partials(
        gathered, both[-1:], head_weight, far_head_weight, x_at, y_at, core_at, side
    )
    upper = summed_along(upper, "mp_0").astype(jnp.bfloat16)
    lower = summed_along(lower, "mp_1").astype(jnp.bfloat16)
    upper = summed_along([upper[k] for k in range(side)], "mp_1")
    lower = summed_along([lower[k] for k in range(side)], "mp_0")

    def rescaled(total):
        half = seqs // 2
        squares = total[half, :half] + total[half, half : 2 * half]
        return total[:half] * lax.rsqrt(squares / full_width + EPS)[:, None]

    logits = jnp.concatenate([rescaled(upper), rescaled(lower)], axis=0)

    local_top = jnp.max(logits, axis=1)
    local_sum = jnp.sum(jnp.exp(logits - local_top[:, None]), axis=1)
    highest, summed = joined_all(local_top, local_sum, (MP, "batch"))
    return (logits, jnp.log(summed) + highest)


def solution(mesh):
    torus = Mesh(
        mesh.devices.reshape(mesh.shape["batch"], 4, 4, 2), ("batch", "mp_0", "mp_1", "mp_2")
    )
    in_specs = (
        P(None, MP),
        P(MP),
        P("batch"),
        P(MP, "batch"),
        P("batch", MP),
        P(None, "batch", MP, None, None),
        P(MP, None),
        P(MP),
        P(MP),
        P(MP, "batch"),
    )
    out_specs = (P(None, BATCH_MP), P())

    def step(*args):
        return local(*args)

    step = jax.shard_map(step, mesh=torus, in_specs=in_specs, out_specs=out_specs, check_vma=False)
    return step
```

time: 168 us -> 156 us (0.929)
  Pallas kernels: 9.25 us -> 16.9 us
  waiting for transfers between devices: 58.2 us -> 65.6 us
  starting transfers between devices: 45.2 us -> 38.4 us
  blocking collectives: 29.9 us -> 23.4 us
  matrix products: 7.31 us -> 0.97 us
  other arithmetic: 12.6 us -> 7.46 us
  local copies, waits for them, and re-layouts: 3.62 us -> 1.55 us
    all_to_all x1 -> x2, waiting for transfers between devices: 8.31 us -> 18.1 us  [the longest x1 10.4 us: local(): parts = lax.all_to_all(parts, MP, split_axis=0, concat_axis=0, tiled=True)]
    pallas_call x1 -> x3, Pallas kernels: 9.25 us -> 16.9 us  [the longest x1 8.75 us: head_partials(): pl.pallas_call(head_block, in_specs=[pl.BlockSpec(memory_space=pltpu.SMEM...]
    all_to_all x2 -> x1, waiting for transfers between devices: 18.1 us -> 11.2 us  [sent_to_all(): lax.all_to_all(jnp.broadcast_to(x[None], (length, *x.shape)), axis, 0, 0,...]
    all_to_all x1 -> x2, blocking collectives: 29.9 us -> 23.4 us  [sent_to_all(): lax.all_to_all(jnp.broadcast_to(x[None], (length, *x.shape)), axis, 0, 0,...]
    dot_general x7 -> x1, matrix products: 7.31 us -> 0.97 us  [local(): jnp.dot(mine, both_out, preferred_element_type=jnp.float32)]
    ppermute x21 -> x15, waiting for transfers between devices: 24 us -> 28.4 us  [shifted(): lax.ppermute(x, axis, [(k, (k + by) % length) for k in range(length)])]
    ppermute x21 -> x15, starting transfers between devices: 18.7 us -> 14.9 us  [shifted(): lax.ppermute(x, axis, [(k, (k + by) % length) for k in range(length)])]
    all_to_all x2 -> x1, starting transfers between devices: 9.8 us -> 6.27 us  [sent_to_all(): lax.all_to_all(jnp.broadcast_to(x[None], (length, *x.shape)), axis, 0, 0,...]
  transfers between devices with their start and end apart: 25 -> 19, of which waited for: 13 -> 9; matrix products, arithmetic and copies ran while one was open for 11% -> 5% of each run, Pallas kernels for 6% -> 5%
where the time goes in v1:
time: 156 us; the launch traced here: 155 us
  waiting for transfers between devices  65.6 us (42%)
  starting transfers between devices  38.4 us (25%)
  blocking collectives  23.4 us (15%)
  Pallas kernels  16.9 us (11%)
  other arithmetic  7.46 us (5%)
    ppermute x15, waiting for transfers between devices, shifted(): lax.ppermute(x, axis, [(k, (k + by) % length) for k in range(length)])  28.4 us
    all_to_all x2, blocking collectives, sent_to_all(): lax.all_to_all(jnp.broadcast_to(x[None], (length, *x.shape)), axis, 0, 0,...  23.4 us
    ppermute x15, starting transfers between devices, shifted(): lax.ppermute(x, axis, [(k, (k + by) % length) for k in range(length)])  14.9 us
    all_to_all x1, waiting for transfers between devices, sent_to_all(): lax.all_to_all(jnp.broadcast_to(x[None], (length, *x.shape)), axis, 0, 0,...  11.2 us
    all_to_all x1, waiting for transfers between devices, local(): parts = lax.all_to_all(parts, MP, split_axis=0, concat_axis=0, tiled=True)  10.4 us
    pallas_call x1, Pallas kernels, head_partials(): pl.pallas_call(head_block, in_specs=[pl.BlockSpec(memory_space=pltpu.SMEM...  8.75 us
    all_to_all x1, starting transfers between devices, local(): lax.all_to_all(partial_out.reshape(batches, per_batch * seq_count, -1), '...  8.17 us
    all_to_all x1, waiting for transfers between devices, local(): lax.all_to_all(partial_out.reshape(batches, per_batch * seq_count, -1), '...  7.87 us
  transfers between devices with their start and end apart: 19, of which 9 were waited for; matrix products, arithmetic and copies ran while one was open for 5% of the time, Pallas kernels for 5%

profile of v1, /device:TPU:1, one launch (start us, length us, event | category | flops | bytes accessed | tf_op | source)
XLA Modules:
  0.0 155.3 jit_solution(5883165045209607860)
XLA Ops:
  0.6 3.3 %collective-permute-start.2 = (bf16[256,12288]{1,0:T(8,128)(2,1)}, bf16[256,12288]{1,0:T(8,128)(2,1)}, u32[]{:S(2)}, u32[]{:S(2)}) collective-permute-start(bf16[256,12288]{1,0:T(8,128)(2,1)} %near_weight.1), channel_id=1, source_target_pairs={{0,1},{1,0},{2,3},{3,2},{4,5},{5,4},{6,7},{7,6},{8,9},{9,8},{10,11... | collective-permute-start | bytes 18874376 | tf_op jit(solution)/shard_map/ppermute | solution.py:32
  3.9 0.7 bitcast_convert_fusion.1
  4.7 0.7 pad_maximum_fusion.2
  5.3 0.0 collective-permute-start
  5.4 0.5 collective-permute-start.1
  5.9 2.3 %query_parts.1 = bf16[256,1152]{1,0:T(8,128)(2,1)} custom-call(bf16[256,256]{1,0:T(8,128)(2,1)} %stream.1, f32[1,256]{1,0:T(1,128)} %bitcast.92, bf16[256,1024]{1,0:T(8,128)(2,1)} %weight.1), custom_call_target="tpu_custom_call" | custom-call | tf_op jit(solution)/shard_map/query_parts/pallas_call | solution.py:50
  8.1 5.5 %all-to-all-start = ((bf16[32,8,1152]{2,1,0:T(8,128)(2,1)}), bf16[32,8,1152]{2,1,0:T(8,128)(2,1)S(1)}, u32[]{:S(2)}, u32[]{:S(2)}) async-start(bf16[32,8,1152]{2,1,0:T(8,128)(2,1)} %bitcast.80), calls=%async_computation | async-start | bytes 1179648 | tf_op jit(solution)/shard_map/all_to_all | solution.py:331
  13.7 0.1 broadcast_subtract_fusion
  13.7 0.1 fusion.19
  13.8 0.1 iota_compare_fusion.2
  13.9 0.7 pad_maximum_fusion.5
  14.6 0.2 select_reduce_fusion.1
  14.7 0.7 fusion.13
  15.4 10.4 %all-to-all-done = bf16[32,8,1152]{2,1,0:T(8,128)(2,1)S(1)} async-done(((bf16[32,8,1152]{2,1,0:T(8,128)(2,1)}), bf16[32,8,1152]{2,1,0:T(8,128)(2,1)S(1)}, u32[]{:S(2)}, u32[]{:S(2)}) %all-to-all-start) | async-done | bytes 589856 | tf_op jit(solution)/shard_map/all_to_all | solution.py:331
  25.9 0.7 convert_reduce_fusion.sums
  26.6 5.9 %attend.1 = bf16[16,8,1024]{2,1,0:T(8,128)(2,1)} custom-call(f32[8,1152]{1,0:T(8,128)} %convert_reduce_fusion.sums, f32[1,1024]{1,0:T(1,128)} %bitcast.91, f32[8,128]{1,0:T(8,128)} %get-tuple-element.45.cosines, f32[8,128]{1,0:T(8,128)} %get-tuple-element.46.sines, s32[1,8192]{1,0:T(1,128)} %bitcast.83, bf16[2,1,64,128,128]{4,3,2,1,0:T(8,128)(2,1)} %pages.1), custom_call_target="tpu_custom_call" | custom-call | tf_op jit(solution)/shard_map/attend/pallas_call | solution.py:153
  32.5 3.5 %all-to-all-start.1 = ((bf16[16,8,1024]{2,1,0:T(8,128)(2,1)}), bf16[16,8,1024]{2,1,0:T(8,128)(2,1)S(1)}, u32[]{:S(2)}, u32[]{:S(2)}) async-start(bf16[16,8,1024]{2,1,0:T(8,128)(2,1)} %attend.1), calls=%async_computation.1 | async-start | bytes 524288 | tf_op jit(solution)/shard_map/all_to_all | solution.py:339
  36.0 0.0 collective-permute-done.1
  36.0 0.1 broadcast_select_fusion.1
  36.1 0.0 copy-start.5
  36.1 0.1 pad_maximum_fusion
  36.2 7.7 %all-to-all-done.1 = bf16[16,8,1024]{2,1,0:T(8,128)(2,1)S(1)} async-done(((bf16[16,8,1024]{2,1,0:T(8,128)(2,1)}), bf16[16,8,1024]{2,1,0:T(8,128)(2,1)S(1)}, u32[]{:S(2)}, u32[]{:S(2)}) %all-to-all-start.1) | async-done | bytes 262176 | tf_op jit(solution)/shard_map/all_to_all | solution.py:339
  43.9 1.0 convolution_convert_fusion
  44.9 8.2 %all-to-all-start.2 = ((bf16[8,16,512]{2,1,0:T(8,128)(2,1)}), bf16[8,16,512]{2,1,0:T(8,128)(2,1)S(1)}, u32[]{:S(2)}, u32[]{:S(2)}) async-start(bf16[8,16,512]{2,1,0:T(8,128)(2,1)} %bitcast.12), calls=%async_computation.2 | async-start | bytes 262144 | tf_op jit(solution)/shard_map/all_to_all | solution.py:350
  53.1 7.9 %all-to-all-done.2 = bf16[8,16,512]{2,1,0:T(8,128)(2,1)S(1)} async-done(((bf16[8,16,512]{2,1,0:T(8,128)(2,1)}), bf16[8,16,512]{2,1,0:T(8,128)(2,1)S(1)}, u32[]{:S(2)}, u32[]{:S(2)}) %all-to-all-start.2) | async-done | bytes 131104 | tf_op jit(solution)/shard_map/all_to_all | solution.py:350
  61.0 0.7 broadcast_in_dim.54
  61.7 6.3 %all-to-all-start.3 = ((bf16[16,16,512]{2,1,0:T(8,128)(2,1)}), bf16[16,16,512]{2,1,0:T(8,128)(2,1)S(1)}, u32[]{:S(2)}, u32[]{:S(2)}) async-start(bf16[16,16,512]{2,1,0:T(8,128)(2,1)} %broadcast_in_dim.54), calls=%async_computation.3 | async-start | bytes 524288 | tf_op jit(solution)/shard_map/all_to_all | solution.py:27
  68.0 0.6 pad_add_fusion.place
  68.6 11.2 %all-to-all-done.3 = bf16[16,16,512]{2,1,0:T(8,128)(2,1)S(1)} async-done(((bf16[16,16,512]{2,1,0:T(8,128)(2,1)}), bf16[16,16,512]{2,1,0:T(8,128)(2,1)S(1)}, u32[]{:S(2)}, u32[]{:S(2)}) %all-to-all-start.3) | async-done | bytes 262176 | tf_op jit(solution)/shard_map/all_to_all | solution.py:27
  79.8 0.7 copy-done.1
  80.5 8.7 %head_partials.1 = (bf16[4,136,384]{2,1,0:T(8,128)(2,1)}, bf16[4,136,384]{2,1,0:T(8,128)(2,1)}, bf16[4,136,384]{2,1,0:T(8,128)(2,1)}, bf16[4,136,384]{2,1,0:T(8,...) custom-call(s32[3]{0:T(128)} %pad_add_fusion.place, ...), custom_call_target="tpu_custom_call" | custom-call | tf_op jit(solution)/shard_map/head_partials/pallas_call | solution.py:256
  89.2 0.1 collective-permute-start.3
  89.3 1.9 %collective-permute-start.4 = (bf16[4,136,384]{2,1,0:T(8,128)(2,1)}, bf16[4,136,384]{2,1,0:T(8,128)(2,1)S(1)}, u32[]{:S(2)}, u32[]{:S(2)}) collective-permute-start(bf16[4,136,384]{2,1,0:T(8,128)(2,1)} %get-tuple-element.12), channel_id=1, source_target_pairs={{0,16},{8,24},{16,0},{24,8},{1,17},{9,25},{17,1},{25,9},{2,18},{10... | collective-permute-start | bytes 1253384 | tf_op jit(solution)/shard_map/ppermute | solution.py:32
  91.2 1.1 collective-permute-start.5
  92.4 0.1 collective-permute-start.9
  92.5 1.7 %collective-permute-start.10 = (bf16[4,136,384]{2,1,0:T(8,128)(2,1)}, bf16[4,136,384]{2,1,0:T(8,128)(2,1)S(1)}, u32[]{:S(2)}, u32[]{:S(2)}) collective-permute-start(bf16[4,136,384]{2,1,0:T(8,128)(2,1)} %get-tuple-element.16), channel_id=1, source_target_pairs={{0,4},{2,6},{4,0},{6,2},{1,5},{3,7},{5,1},{7,3},{8,12},{10,14},{12... | collective-permute-start | bytes 1253384 | tf_op jit(solution)/shard_map/ppermute | solution.py:32
  94.2 17.0 %collective-permute-done.3 = bf16[4,136,384]{2,1,0:T(8,128)(2,1)S(1)} collective-permute-done((bf16[4,136,384]{2,1,0:T(8,128)(2,1)}, bf16[4,136,384]{2,1,0:T(8,128)(2,1)S(1)}, u32[]{:S(2)}, u32[]{:S(2)}) %collective-permute-start.3) | collective-permute-done | bytes 417824 | tf_op jit(solution)/shard_map/ppermute | solution.py:32
  111.2 0.5 collective-permute-start.11
  111.7 0.0 collective-permute-done.5
  111.8 1.2 add_convert_fusion.1
  113.0 1.0 collective-permute-start.6
  114.1 1.7 %collective-permute-start.8 = (bf16[136,384]{1,0:T(8,128)(2,1)S(1)}, bf16[136,384]{1,0:T(8,128)(2,1)S(1)}, u32[]{:S(2)}, u32[]{:S(2)}) collective-permute-start(bf16[136,384]{1,0:T(8,128)(2,1)S(1)} %get-tuple-element.25), channel_id=1, source_target_pairs={{0,6},{2,0},{4,2},{6,4},{1,7},{3,1},{5,3},{7,5},{8,14},{10,8},{12,... | collective-permute-start | bytes 313352 | tf_op jit(solution)/shard_map/ppermute | solution.py:32
  115.8 0.1 collective-permute-start.7
  115.9 0.0 collective-permute-done.10
  115.9 6.4 %collective-permute-done.11 = bf16[4,136,384]{2,1,0:T(8,128)(2,1)S(1)} collective-permute-done((bf16[4,136,384]{2,1,0:T(8,128)(2,1)}, bf16[4,136,384]{2,1,0:T(8,128)(2,1)S(1)}, u32[]{:S(2)}, u32[]{:S(2)}) %collective-permute-start.11) | collective-permute-done | bytes 417824 | tf_op jit(solution)/shard_map/ppermute | solution.py:32
  122.4 0.2 add_convert_fusion
  122.6 0.1 collective-permute-start.12
  122.7 2.7 %collective-permute-start.14 = (bf16[136,384]{1,0:T(8,128)(2,1)S(1)}, bf16[136,384]{1,0:T(8,128)(2,1)S(1)}, u32[]{:S(2)}, u32[]{:S(2)}) collective-permute-start(bf16[136,384]{1,0:T(8,128)(2,1)S(1)} %get-tuple-element.28), channel_id=1, source_target_pairs={{0,24},{8,0},{16,8},{24,16},{1,25},{9,1},{17,9},{25,17},{2,26},{10... | collective-permute-start | bytes 313352 | tf_op jit(solution)/shard_map/ppermute | solution.py:32
  125.4 0.0 collective-permute-done.8
  125.4 0.0 collective-permute-done.7
  125.4 0.1 fusion.4
  125.5 0.1 slice_multiply_fusion.1
  125.6 1.9 %collective-permute-done.12 = bf16[136,384]{1,0:T(8,128)(2,1)S(1)} collective-permute-done((bf16[136,384]{1,0:T(8,128)(2,1)S(1)}, bf16[136,384]{1,0:T(8,128)(2,1)S(1)}, u32[]{:S(2)}, u32[]{:S(2)}) %collective-permute-start.12) | collective-permute-done | bytes 104480 | tf_op jit(solution)/shard_map/ppermute | solution.py:32
  127.4 0.7 collective-permute-done.14
  128.1 2.4 %collective-permute-done.13 = bf16[136,384]{1,0:T(8,128)(2,1)S(1)} collective-permute-done((bf16[136,384]{1,0:T(8,128)(2,1)S(1)}, bf16[136,384]{1,0:T(8,128)(2,1)S(1)}, u32[]{:S(2)}, u32[]{:S(2)}) %collective-permute-start.13) | collective-permute-done | bytes 104480 | tf_op jit(solution)/shard_map/ppermute | solution.py:32
  130.5 0.1 fusion.2
  130.6 0.1 slice_multiply_fusion
  130.7 0.1 fusion.22
  130.8 0.0 copy-start
  130.8 0.2 exponential_reduce_fusion
  131.1 14.4 %all_to_all.30 = f32[32,2,256]{2,1,0:T(2,128)S(1)} all-to-all(f32[32,2,256]{2,1,0:T(2,128)S(1)} %broadcast_in_dim.55), channel_id=1, replica_groups=mesh['batch'=8,'mp_0'=4,'mp_1'=4,'mp_2'=2] {'mp_0','mp_1','mp_2'}, dimensions={0} | all-to-all | bytes 131072 | tf_op jit(solution)/shard_map/all_to_all | solution.py:27
  145.5 0.1 slice_reduce_fusion.1
  145.6 9.0 %all_to_all.31 = f32[8,2,256]{2,1,0:T(2,128)S(1)} all-to-all(f32[8,2,256]{2,1,0:T(2,128)S(1)} %broadcast_in_dim.56), channel_id=1, replica_groups=mesh['batch'=8,'mp_0'=4,'mp_1'=4,'mp_2'=2] {'batch'}, dimensions={0} | all-to-all | bytes 32768 | tf_op jit(solution)/shard_map/all_to_all | solution.py:27
  154.7 0.6 log_add_fusion
  (37 shorter events, 0.3 us)
Async XLA Ops:
  0.6 13.0 %copy-start.7 = (s32[8]{0:T(128)S(1)}, s32[8]{0:T(128)}, u32[]{:S(2)}) copy-start(s32[8]{0:T(128)} %param.17) | copy-start | bytes 100
  0.6 14.0 %copy-start.6 = (s32[8,24]{1,0:T(8,128)S(1)}, s32[8,24]{1,0:T(8,128)}, u32[]{:S(2)}) copy-start(s32[8,24]{1,0:T(8,128)} %param.16) | copy-start | bytes 2308
  0.6 79.1 %collective-permute-start.2 = (bf16[256,12288]{1,0:T(8,128)(2,1)}, bf16[256,12288]{1,0:T(8,128)(2,1)}, u32[]{:S(2)}, u32[]{:S(2)}) collective-permute-start(bf16[256,12288]{1,0:T(8,128)(2,1)} %near_weight.1), channel_id=1, source_target_pairs={{0,1},{1,0},{2,3},{3,2},{4,5},{5,4},{6,7},{7,6},{8,9},{9,8},{10,11... | collective-permute-start | bytes 18874376 | tf_op jit(solution)/shard_map/ppermute | solution.py:32
  5.3 47.7 %collective-permute-start = (f32[17,256]{1,0:T(8,128)S(1)}, f32[17,256]{1,0:T(8,128)S(1)}, u32[]{:S(2)}, u32[]{:S(2)}) collective-permute-start(f32[17,256]{1,0:T(8,128)S(1)} %pad_maximum_fusion.2), channel_id=1, source_target_pairs={{0,1},{1,0},{2,3},{3,2},{4,5},{5,4},{6,7},{7,6},{8,9},{9,8},{10,11... | collective-permute-start | bytes 52232 | tf_op jit(solution)/shard_map/ppermute | solution.py:32
  5.4 30.6 %collective-permute-start.1 = (bf16[1024,256]{1,0:T(8,128)(2,1)}, bf16[1024,256]{1,0:T(8,128)(2,1)S(1)}, u32[]{:S(2)}, u32[]{:S(2)}) collective-permute-start(bf16[1024,256]{1,0:T(8,128)(2,1)} %param.14), channel_id=1, source_target_pairs={{0,1},{1,0},{2,3},{3,2},{4,5},{5,4},{6,7},{7,6},{8,9},{9,8},{10,11... | collective-permute-start | bytes 1572872 | tf_op jit(solution)/shard_map/ppermute | solution.py:32
  8.1 17.8 %all-to-all-start = ((bf16[32,8,1152]{2,1,0:T(8,128)(2,1)}), bf16[32,8,1152]{2,1,0:T(8,128)(2,1)S(1)}, u32[]{:S(2)}, u32[]{:S(2)}) async-start(bf16[32,8,1152]{2,1,0:T(8,128)(2,1)} %bitcast.80), calls=%async_computation | async-start | bytes 1179648 | tf_op jit(solution)/shard_map/all_to_all | solution.py:331
  26.6 9.5 %copy-start.2 = (bf16[1024,256]{1,0:T(8,128)(2,1)S(1)}, bf16[1024,256]{1,0:T(8,128)(2,1)}, u32[]{:S(2)}) copy-start(bf16[1024,256]{1,0:T(8,128)(2,1)} %param.14) | copy-start | bytes 1572868
  32.5 11.4 %all-to-all-start.1 = ((bf16[16,8,1024]{2,1,0:T(8,128)(2,1)}), bf16[16,8,1024]{2,1,0:T(8,128)(2,1)S(1)}, u32[]{:S(2)}, u32[]{:S(2)}) async-start(bf16[16,8,1024]{2,1,0:T(8,128)(2,1)} %attend.1), calls=%async_computation.1 | async-start | bytes 524288 | tf_op jit(solution)/shard_map/all_to_all | solution.py:339
  36.1 16.9 %copy-start.5 = (f32[256]{0:T(256)S(1)}, f32[256]{0:T(256)}, u32[]{:S(2)}) copy-start(f32[256]{0:T(256)} %param.18) | copy-start | bytes 3076
  44.9 16.1 %all-to-all-start.2 = ((bf16[8,16,512]{2,1,0:T(8,128)(2,1)}), bf16[8,16,512]{2,1,0:T(8,128)(2,1)S(1)}, u32[]{:S(2)}, u32[]{:S(2)}) async-start(bf16[8,16,512]{2,1,0:T(8,128)(2,1)} %bitcast.12), calls=%async_computation.2 | async-start | bytes 262144 | tf_op jit(solution)/shard_map/all_to_all | solution.py:350
  53.1 26.7 %copy-start.4 = (f32[1,512]{1,0:T(1,128)}, f32[1,512]{1,0:T(1,128)S(1)}, u32[]{:S(2)}) copy-start(f32[1,512]{1,0:T(1,128)S(1)} %pad_maximum_fusion.7.gain) | copy-start | bytes 6148
  61.7 18.0 %all-to-all-start.3 = ((bf16[16,16,512]{2,1,0:T(8,128)(2,1)}), bf16[16,16,512]{2,1,0:T(8,128)(2,1)S(1)}, u32[]{:S(2)}, u32[]{:S(2)}) async-start(bf16[16,16,512]{2,1,0:T(8,128)(2,1)} %broadcast_in_dim.54), calls=%async_computation.3 | async-start | bytes 524288 | tf_op jit(solution)/shard_map/all_to_all | solution.py:27
  79.8 0.7 copy-start.1
  89.2 33.1 %copy-start.3 = (bf16[4,136,384]{2,1,0:T(8,128)(2,1)S(1)}, bf16[4,136,384]{2,1,0:T(8,128)(2,1)}, u32[]{:S(2)}) copy-start(bf16[4,136,384]{2,1,0:T(8,128)(2,1)} %get-tuple-element.14) | copy-start | bytes 1253380
  89.2 22.0 %collective-permute-start.3 = (bf16[4,136,384]{2,1,0:T(8,128)(2,1)}, bf16[4,136,384]{2,1,0:T(8,128)(2,1)S(1)}, u32[]{:S(2)}, u32[]{:S(2)}) collective-permute-start(bf16[4,136,384]{2,1,0:T(8,128)(2,1)} %get-tuple-element.11), channel_id=1, source_target_pairs={{0,8},{8,16},{16,24},{24,0},{1,9},{9,17},{17,25},{25,1},{2,10},{10... | collective-permute-start | bytes 1253384 | tf_op jit(solution)/shard_map/ppermute | solution.py:32
  89.3 22.4 %collective-permute-start.4 = (bf16[4,136,384]{2,1,0:T(8,128)(2,1)}, bf16[4,136,384]{2,1,0:T(8,128)(2,1)S(1)}, u32[]{:S(2)}, u32[]{:S(2)}) collective-permute-start(bf16[4,136,384]{2,1,0:T(8,128)(2,1)} %get-tuple-element.12), channel_id=1, source_target_pairs={{0,16},{8,24},{16,0},{24,8},{1,17},{9,25},{17,1},{25,9},{2,18},{10... | collective-permute-start | bytes 1253384 | tf_op jit(solution)/shard_map/ppermute | solution.py:32
  91.2 20.5 %collective-permute-start.5 = (bf16[4,136,384]{2,1,0:T(8,128)(2,1)}, bf16[4,136,384]{2,1,0:T(8,128)(2,1)S(1)}, u32[]{:S(2)}, u32[]{:S(2)}) collective-permute-start(bf16[4,136,384]{2,1,0:T(8,128)(2,1)} %get-tuple-element.13), channel_id=1, source_target_pairs={{0,24},{8,0},{16,8},{24,16},{1,25},{9,1},{17,9},{25,17},{2,26},{10... | collective-permute-start | bytes 1253384 | tf_op jit(solution)/shard_map/ppermute | solution.py:32
  92.4 23.4 %collective-permute-start.9 = (bf16[4,136,384]{2,1,0:T(8,128)(2,1)}, bf16[4,136,384]{2,1,0:T(8,128)(2,1)S(1)}, u32[]{:S(2)}, u32[]{:S(2)}) collective-permute-start(bf16[4,136,384]{2,1,0:T(8,128)(2,1)} %get-tuple-element.15), channel_id=1, source_target_pairs={{0,2},{2,4},{4,6},{6,0},{1,3},{3,5},{5,7},{7,1},{8,10},{10,12},{12... | collective-permute-start | bytes 1253384 | tf_op jit(solution)/shard_map/ppermute | solution.py:32
  92.5 23.4 %collective-permute-start.10 = (bf16[4,136,384]{2,1,0:T(8,128)(2,1)}, bf16[4,136,384]{2,1,0:T(8,128)(2,1)S(1)}, u32[]{:S(2)}, u32[]{:S(2)}) collective-permute-start(bf16[4,136,384]{2,1,0:T(8,128)(2,1)} %get-tuple-element.16), channel_id=1, source_target_pairs={{0,4},{2,6},{4,0},{6,2},{1,5},{3,7},{5,1},{7,3},{8,12},{10,14},{12... | collective-permute-start | bytes 1253384 | tf_op jit(solution)/shard_map/ppermute | solution.py:32
  111.2 11.1 %collective-permute-start.11 = (bf16[4,136,384]{2,1,0:T(8,128)(2,1)}, bf16[4,136,384]{2,1,0:T(8,128)(2,1)S(1)}, u32[]{:S(2)}, u32[]{:S(2)}) collective-permute-start(bf16[4,136,384]{2,1,0:T(8,128)(2,1)} %get-tuple-element.17), channel_id=1, source_target_pairs={{0,6},{2,0},{4,2},{6,4},{1,7},{3,1},{5,3},{7,5},{8,14},{10,8},{12,... | collective-permute-start | bytes 1253384 | tf_op jit(solution)/shard_map/ppermute | solution.py:32
  113.0 12.3 %collective-permute-start.6 = (bf16[136,384]{1,0:T(8,128)(2,1)S(1)}, bf16[136,384]{1,0:T(8,128)(2,1)S(1)}, u32[]{:S(2)}, u32[]{:S(2)}) collective-permute-start(bf16[136,384]{1,0:T(8,128)(2,1)S(1)} %get-tuple-element.24), channel_id=1, source_target_pairs={{0,2},{2,4},{4,6},{6,0},{1,3},{3,5},{5,7},{7,1},{8,10},{10,12},{12... | collective-permute-start | bytes 313352 | tf_op jit(solution)/shard_map/ppermute | solution.py:32
  114.1 11.3 %collective-permute-start.8 = (bf16[136,384]{1,0:T(8,128)(2,1)S(1)}, bf16[136,384]{1,0:T(8,128)(2,1)S(1)}, u32[]{:S(2)}, u32[]{:S(2)}) collective-permute-start(bf16[136,384]{1,0:T(8,128)(2,1)S(1)} %get-tuple-element.25), channel_id=1, source_target_pairs={{0,6},{2,0},{4,2},{6,4},{1,7},{3,1},{5,3},{7,5},{8,14},{10,8},{12,... | collective-permute-start | bytes 313352 | tf_op jit(solution)/shard_map/ppermute | solution.py:32
  115.8 9.6 %collective-permute-start.7 = (bf16[136,384]{1,0:T(8,128)(2,1)S(1)}, bf16[136,384]{1,0:T(8,128)(2,1)S(1)}, u32[]{:S(2)}, u32[]{:S(2)}) collective-permute-start(bf16[136,384]{1,0:T(8,128)(2,1)S(1)} %get-tuple-element.26), channel_id=1, source_target_pairs={{0,4},{2,6},{4,0},{6,2},{1,5},{3,7},{5,1},{7,3},{8,12},{10,14},{12... | collective-permute-start | bytes 313352 | tf_op jit(solution)/shard_map/ppermute | solution.py:32
  122.6 4.8 %collective-permute-start.12 = (bf16[136,384]{1,0:T(8,128)(2,1)S(1)}, bf16[136,384]{1,0:T(8,128)(2,1)S(1)}, u32[]{:S(2)}, u32[]{:S(2)}) collective-permute-start(bf16[136,384]{1,0:T(8,128)(2,1)S(1)} %get-tuple-element.27), channel_id=1, source_target_pairs={{0,8},{8,16},{16,24},{24,0},{1,9},{9,17},{17,25},{25,1},{2,10},{10... | collective-permute-start | bytes 313352 | tf_op jit(solution)/shard_map/ppermute | solution.py:32
  122.7 5.4 %collective-permute-start.14 = (bf16[136,384]{1,0:T(8,128)(2,1)S(1)}, bf16[136,384]{1,0:T(8,128)(2,1)S(1)}, u32[]{:S(2)}, u32[]{:S(2)}) collective-permute-start(bf16[136,384]{1,0:T(8,128)(2,1)S(1)} %get-tuple-element.28), channel_id=1, source_target_pairs={{0,24},{8,0},{16,8},{24,16},{1,25},{9,1},{17,9},{25,17},{2,26},{10... | collective-permute-start | bytes 313352 | tf_op jit(solution)/shard_map/ppermute | solution.py:32
  125.4 5.1 %collective-permute-start.13 = (bf16[136,384]{1,0:T(8,128)(2,1)S(1)}, bf16[136,384]{1,0:T(8,128)(2,1)S(1)}, u32[]{:S(2)}, u32[]{:S(2)}) collective-permute-start(bf16[136,384]{1,0:T(8,128)(2,1)S(1)} %get-tuple-element.29), channel_id=1, source_target_pairs={{0,16},{8,24},{16,0},{24,8},{1,17},{9,25},{17,1},{25,9},{2,18},{10... | collective-permute-start | bytes 313352 | tf_op jit(solution)/shard_map/ppermute | solution.py:32
  130.8 24.5 %copy-start = (f32[256,384]{1,0:T(8,128)}, f32[256,384]{1,0:T(8,128)S(1)}, u32[]{:S(2)}) copy-start(f32[256,384]{1,0:T(8,128)S(1)} %get-tuple-element.21) | copy-start | bytes 1179652

commit v2 on v1

--- a/solution.py
+++ b/solution.py
@@ -20,6 +20,16 @@
 INTERPRET = False
 
 LANES = 128
+HEAD_VMEM = 24 * 2**20
+ATTEND_VMEM = 16 * 2**20
+
+
+def near_by(x):
+    return pltpu.with_memory_space_constraint(x, pltpu.VMEM)
+
+
+def far_off(x):
+    return pltpu.with_memory_space_constraint(x, pltpu.HBM)
 
 
 def sent_to_all(x, axis):
@@ -49,7 +59,7 @@
 def query_parts(stream, gain, weight):
     return pl.pallas_call(
         query_block,
-        out_shape=jax.ShapeDtypeStruct((stream.shape[0], weight.shape[1] + LANES), jnp.bfloat16),
+        out_shape=pltpu.VMEM((stream.shape[0], weight.shape[1] + LANES), jnp.bfloat16),
         interpret=INTERPRET,
         name="query_parts",
     )(stream, gain[None], weight)
@@ -83,39 +93,42 @@
     return jnp.where(at[None, :] < visible[:, None], owner[:, None], -1)
 
 
-def attend_block(full_width, sums, bias, cosines, sines, owners, pages, out, *scratch):
+def attend_block(full_width, chunks, sums, table, owners, pages, out, *scratch):
     keys, values, scores, sems = scratch
     copies, seq_count, width = out.shape
     pool_size, page_size, head_size = keys.shape
     heads = width // head_size
     rows = heads * seq_count
-    chunks = sems.shape[1]
+    fetched = pool_size // sems.shape[1]
     slots = pool_size // chunks
     tokens = slots * page_size
 
     fetches = []
     for kind, held in enumerate((keys, values)):
-        for k in range(chunks):
-            at = pl.ds(k * slots, slots)
+        for k in range(pool_size // fetched):
+            at = pl.ds(k * fetched, fetched)
             copy = pltpu.make_async_copy(pages.at[kind, 0, at], held.at[at], sems.at[kind, k])
             copy.start()
             fetches.append(copy)
 
+    bias, cosines = table[:, :width], table[:, width : width + head_size]
+    sines = table[:, width + head_size :]
     tail = sums[:, width:]
     lane = lax.broadcasted_iota(jnp.int32, tail.shape, 1)
     squares = jnp.sum(jnp.where(lane < 2, tail, 0.0), axis=1, keepdims=True)
-    turned = sums[:, :width] * lax.rsqrt(squares / full_width + EPS) + bias[...]
+    turned = sums[:, :width] * lax.rsqrt(squares / full_width + EPS) + bias
     pieces = []
     for k in range(heads):
         piece = turned[:, k * head_size : (k + 1) * head_size]
         across = pltpu.roll(piece, head_size // 2, 1)
-        pieces.append(piece * cosines[...] + across * sines[...])
+        pieces.append(piece * cosines + across * sines)
     queries = jnp.concatenate(pieces, axis=0).astype(jnp.bfloat16)
 
     row_seq = lax.broadcasted_iota(jnp.int32, (rows, 1), 0) % seq_count
     highest = jnp.full((rows, head_size), -1e30, jnp.float32)
     for k in range(chunks):
-        fetches[k].wait()
+        if k * slots % fetched == 0:
+            fetches[k * slots // fetched].wait()
         key = keys[k * slots : (k + 1) * slots].reshape(tokens, head_size)
         here = lax.dot_general(
             queries, key, (((1,), (1,)), ((), ())), preferred_element_type=jnp.float32
@@ -132,7 +145,8 @@
         powers = jnp.exp(scores[:, k * tokens : (k + 1) * tokens] - highest)
         for t in range(tokens // head_size):
             summed += powers[:, t * head_size : (t + 1) * head_size]
-        fetches[chunks + k].wait()
+        if k * slots % fetched == 0:
+            fetches[pool_size // fetched + k * slots // fetched].wait()
         value = values[k * slots : (k + 1) * slots].reshape(tokens, head_size)
         mixed += jnp.dot(powers.astype(jnp.bfloat16), value, preferred_element_type=jnp.float32)
     result = mixed / jnp.sum(summed, axis=1, keepdims=True)
@@ -142,7 +156,7 @@
         out[k] = row
 
 
-def attend(sums, bias, cosines, sines, owners, page_cache, full_width, copies, chunks=8):
+def attend(sums, table, owners, page_cache, full_width, copies, fetches=1, chunks=4):
     seq_count, width = sums.shape
     width -= LANES
     pool_size, page_size, head_size = page_cache.shape[2:]
@@ -151,28 +165,27 @@
     in_hbm = pl.BlockSpec(memory_space=pltpu.HBM)
     in_vmem = pl.BlockSpec(memory_space=pltpu.VMEM)
     return pl.pallas_call(
-        functools.partial(attend_block, full_width),
-        in_specs=[in_vmem, in_vmem, in_vmem, in_vmem, in_vmem, in_hbm],
+        functools.partial(attend_block, full_width, chunks),
+        in_specs=[in_vmem, in_vmem, in_vmem, in_hbm],
         out_specs=in_vmem,
-        out_shape=jax.ShapeDtypeStruct((copies, seq_count, width), jnp.bfloat16),
+        out_shape=pltpu.VMEM((copies, seq_count, width), jnp.bfloat16),
         scratch_shapes=[
             pltpu.VMEM(pool, jnp.bfloat16),
             pltpu.VMEM(pool, jnp.bfloat16),
             pltpu.VMEM((rows, pool_size * page_size), jnp.float32),
-            pltpu.SemaphoreType.DMA((2, chunks)),
+            pltpu.SemaphoreType.DMA((2, fetches)),
         ],
+        compiler_params=pltpu.CompilerParams(vmem_limit_bytes=ATTEND_VMEM),
         interpret=INTERPRET,
         name="attend",
-    )(sums, bias[None], cosines, sines, owners.reshape(1, -1), page_cache)
-
-
-def head_block(place, gain, gathered_far, near_weight, far_weight, *refs):
-    batches, cores, per_batch, _, depth = gathered_far.shape
-    side = (len(refs) - 7) // 2
+    )(near_by(sums), near_by(table), near_by(owners.reshape(1, -1)), far_off(page_cache))
+
+
+def head_block(place, gathered, gain, near_weight, far_weight, *refs):
+    batches, cores, per_batch, _, depth = gathered.shape
+    side = (len(refs) - 2) // 2
     out_x, out_y = refs[:side], refs[side : 2 * side]
-    gathered, weights, block_x, block_y, sem, sems_in, sems_out = refs[2 * side :]
-    fetch = pltpu.make_async_copy(gathered_far, gathered, sem)
-    fetch.start()
+    weights, sems_in = refs[2 * side :]
     x_at, y_at, core_at = place[0], place[1], place[2]
     width = near_weight.shape[1] // (side * side * cores)
     rows_here = depth // cores
@@ -197,7 +210,6 @@
         for copy in copies:
             copy.start()
 
-    fetch.wait()
     pieces = [
         gathered[b, c, i].astype(jnp.float32)
         for b in range(batches)
@@ -207,44 +219,32 @@
     ordered = jnp.concatenate(pieces, axis=0)
     features = ordered.astype(jnp.bfloat16)
     half = ordered.shape[0] // 2
-    unscaled = ordered / gain[...]
-    extra = block_x.shape[2] - half
-    squares = lax.dot_general(
-        jnp.ones((extra, depth), jnp.float32),
-        unscaled * unscaled,
-        (((1,), (1,)), ((), ())),
-        precision=lax.Precision.HIGHEST,
-        preferred_element_type=jnp.float32,
-    )
-    coarse = squares.astype(jnp.bfloat16)
-    fine = (squares - coarse.astype(jnp.float32)).astype(jnp.bfloat16)
-    filler = jnp.zeros((extra, width - 2 * half), jnp.bfloat16)
-    tail_x = jnp.concatenate([coarse[:, :half], fine[:, :half], filler], axis=1)
-    tail_y = jnp.concatenate([coarse[:, half:], fine[:, half:], filler], axis=1)
-
-    stores = []
+    extra = out_x[0].shape[1] - half
+    unscaled = ordered * (1.0 / gain[...])
+    squares = jnp.sum(unscaled * unscaled, axis=1, keepdims=True)
+    diagonal = lax.broadcasted_iota(jnp.int32, (half, half), 0) == lax.broadcasted_iota(
+        jnp.int32, (half, half), 1
+    )
+    tails = []
+    for part in (squares[:half], squares[half:]):
+        line = jnp.sum(jnp.where(diagonal, part, 0.0), axis=0, keepdims=True)
+        line = jnp.broadcast_to(line, (extra, half))
+        coarse = line.astype(jnp.bfloat16)
+        fine = (line - coarse.astype(jnp.float32)).astype(jnp.bfloat16)
+        filler = jnp.zeros((extra, width - 2 * half), jnp.bfloat16)
+        tails.append(jnp.concatenate([coarse, fine, filler], axis=1))
+    tail_x, tail_y = tails
+
     for x_to in range(side):
         for copy in loads[x_to]:
             copy.wait()
         product = jnp.dot(features, weights[x_to], preferred_element_type=jnp.float32)
         for y_to in range(side):
             part = product[:, y_to * width : (y_to + 1) * width].astype(jnp.bfloat16)
-            block_x[x_to, y_to, :half] = part[:half]
-            block_x[x_to, y_to, half:] = tail_x
-            block_y[y_to, x_to, :half] = part[half:]
-            block_y[y_to, x_to, half:] = tail_y
-            for copy in (
-                pltpu.make_async_copy(
-                    block_x.at[x_to, y_to], out_x[x_to].at[y_to], sems_out.at[0, x_to, y_to]
-                ),
-                pltpu.make_async_copy(
-                    block_y.at[y_to, x_to], out_y[y_to].at[x_to], sems_out.at[1, x_to, y_to]
-                ),
-            ):
-                copy.start()
-                stores.append(copy)
-    for copy in stores:
-        copy.wait()
+            out_x[x_to][y_to, :half] = part[:half]
+            out_x[x_to][y_to, half:] = tail_x
+            out_y[y_to][x_to, :half] = part[half:]
+            out_y[y_to][x_to, half:] = tail_y
 
 
 def head_partials(gathered, gain, near_weight, far_weight, x_at, y_at, core_at, side):
@@ -258,29 +258,24 @@
         in_specs=[
             pl.BlockSpec(memory_space=pltpu.SMEM),
             pl.BlockSpec(memory_space=pltpu.VMEM),
-            in_hbm,
+            pl.BlockSpec(memory_space=pltpu.VMEM),
             in_hbm,
             in_hbm,
         ],
-        out_specs=[in_hbm] * (2 * side),
-        out_shape=[jax.ShapeDtypeStruct(block, jnp.bfloat16)] * (2 * side),
+        out_shape=[pltpu.VMEM(block, jnp.bfloat16)] * (2 * side),
         scratch_shapes=[
-            pltpu.VMEM(gathered.shape, jnp.bfloat16),
             pltpu.VMEM((side, depth, side * width), jnp.bfloat16),
-            pltpu.VMEM((side, *block), jnp.bfloat16),
-            pltpu.VMEM((side, *block), jnp.bfloat16),
-            pltpu.SemaphoreType.DMA,
             pltpu.SemaphoreType.DMA((side, 2 * side)),
-            pltpu.SemaphoreType.DMA((2, side, side)),
         ],
+        compiler_params=pltpu.CompilerParams(vmem_limit_bytes=HEAD_VMEM),
         interpret=INTERPRET,
         name="head_partials",
     )(
         jnp.stack([x_at, y_at, core_at]).astype(jnp.int32),
-        gain,
-        gathered,
-        near_weight,
-        far_weight,
+        near_by(gathered),
+        near_by(gain),
+        far_off(near_weight),
+        far_off(far_weight),
     )
     return outs[:side], outs[side:]
 
@@ -331,9 +326,11 @@
     parts = lax.all_to_all(parts, MP, split_axis=0, concat_axis=0, tiled=True)
     owners = token_owners(page_table, lengths, *page_cache.shape[2:4])
     cosines, sines = turns(lengths - 1, head_size)
+    bias = jnp.broadcast_to(query_bias[None], (seq_count, query_bias.shape[0]))
+    table = jnp.concatenate([bias, cosines, sines], axis=1)
     sums = jnp.sum(parts.astype(jnp.float32), axis=0)
     attended = attend(
-        sums, query_bias, cosines, sines, owners, page_cache, full_width, side * side
+        sums, table, owners, page_cache, full_width, side * side
     )
 
     mine = lax.all_to_all(attended, XY, 0, 0, tiled=True).reshape(side * side * seq_count, -1)

time: 156 us -> 148 us (0.949)
  Pallas kernels: 16.9 us -> 10.9 us
  other arithmetic: 7.46 us -> 4.08 us
  waiting for transfers between devices: 65.6 us -> 67.7 us
    pallas_call x1, Pallas kernels: 8.75 us -> 4.72 us  [head_partials(): pl.pallas_call(head_block, in_specs=[pl.BlockSpec(memory_space=pltpu.SMEM...]
    pallas_call x2, Pallas kernels: 8.13 us -> 6.15 us  [the longest x1 3.88 us: attend(): pl.pallas_call(functools.partial(attend_block, full_width, chunks), in_sp...]
  transfers between devices with their start and end apart: 19 -> 19, of which waited for: 9 -> 9; matrix products, arithmetic and copies ran while one was open for 5% -> 3% of each run, Pallas kernels for 5% -> 4%
where the time goes in v2:
time: 148 us
  waiting for transfers between devices  67.7 us (46%)
  starting transfers between devices  38.6 us (26%)
  blocking collectives  23.4 us (16%)
  Pallas kernels  10.9 us (7%)
  other arithmetic  4.08 us (3%)
    ppermute x15, waiting for transfers between devices, shifted(): lax.ppermute(x, axis, [(k, (k + by) % length) for k in range(length)])  28.9 us
    all_to_all x2, blocking collectives, sent_to_all(): lax.all_to_all(jnp.broadcast_to(x[None], (length, *x.shape)), axis, 0, 0,...  23.4 us
    ppermute x15, starting transfers between devices, shifted(): lax.ppermute(x, axis, [(k, (k + by) % length) for k in range(length)])  15.1 us
    all_to_all x1, waiting for transfers between devices, sent_to_all(): lax.all_to_all(jnp.broadcast_to(x[None], (length, *x.shape)), axis, 0, 0,...  11.7 us
    all_to_all x1, waiting for transfers between devices, local(): parts = lax.all_to_all(parts, MP, split_axis=0, concat_axis=0, tiled=True)  11.6 us
    all_to_all x1, starting transfers between devices, local(): lax.all_to_all(partial_out.reshape(batches, per_batch * seq_count, -1), '...  8.18 us
    all_to_all x1, waiting for transfers between devices, local(): lax.all_to_all(partial_out.reshape(batches, per_batch * seq_count, -1), '...  7.88 us
    all_to_all x1, waiting for transfers between devices, local(): lax.all_to_all(attended, XY, 0, 0, tiled=True)  7.68 us
  transfers between devices with their start and end apart: 19, of which 9 were waited for; matrix products, arithmetic and copies ran while one was open for 3% of the time, Pallas kernels for 4%

profile of v2, /device:TPU:1, one launch (start us, length us, event | category | flops | bytes accessed | tf_op | source)
XLA Modules:
  0.0 147.5 jit_solution(7801879536738310337)
XLA Ops:
  0.7 3.3 %collective-permute-start.2 = (bf16[256,12288]{1,0:T(8,128)(2,1)}, bf16[256,12288]{1,0:T(8,128)(2,1)}, u32[]{:S(2)}, u32[]{:S(2)}) collective-permute-start(bf16[256,12288]{1,0:T(8,128)(2,1)} %near_weight.1), channel_id=1, source_target_pairs={{0,1},{1,0},{2,3},{3,2},{4,5},{5,4},{6,7},{7,6},{8,9},{9,8},{10,11... | collective-permute-start | bytes 18874376 | tf_op jit(solution)/shard_map/ppermute | solution.py:42
  3.9 0.7 bitcast_convert_fusion.1
  4.7 0.7 pad_maximum_fusion.2
  5.3 0.0 collective-permute-start
  5.4 0.5 collective-permute-start.1
  5.9 2.3 %query_parts.1 = bf16[256,1152]{1,0:T(8,128)(2,1)} custom-call(bf16[256,256]{1,0:T(8,128)(2,1)} %stream.1, f32[1,256]{1,0:T(1,128)} %bitcast.89, bf16[256,1024]{1,0:T(8,128)(2,1)} %weight.1), custom_call_target="tpu_custom_call" | custom-call | tf_op jit(solution)/shard_map/query_parts/pallas_call | solution.py:60
  8.1 5.5 %all-to-all-start = ((bf16[32,8,1152]{2,1,0:T(8,128)(2,1)}), bf16[32,8,1152]{2,1,0:T(8,128)(2,1)S(1)}, u32[]{:S(2)}, u32[]{:S(2)}) async-start(bf16[32,8,1152]{2,1,0:T(8,128)(2,1)} %bitcast.8), calls=%async_computation | async-start | bytes 1179648 | tf_op jit(solution)/shard_map/all_to_all | solution.py:326
  13.7 0.1 multiply_sine_fusion
  13.8 0.1 broadcast_subtract_fusion
  13.9 0.1 iota_compare_fusion.2
  13.9 0.1 concatenate.21.table
  14.0 0.2 select_reduce_fusion.1
  14.2 0.1 fusion.14
  14.3 11.6 %all-to-all-done = bf16[32,8,1152]{2,1,0:T(8,128)(2,1)S(1)} async-done(((bf16[32,8,1152]{2,1,0:T(8,128)(2,1)}), bf16[32,8,1152]{2,1,0:T(8,128)(2,1)S(1)}, u32[]{:S(2)}, u32[]{:S(2)}) %all-to-all-start) | async-done | bytes 589856 | tf_op jit(solution)/shard_map/all_to_all | solution.py:326
  25.9 0.1 convert_reduce_fusion.sums
  26.0 0.0 copy-start.1
  26.0 3.9 %attend.1 = bf16[16,8,1024]{2,1,0:T(8,128)(2,1)} custom-call(f32[8,1152]{1,0:T(8,128)S(1)} %convert_reduce_fusion.sums, f32[8,1280]{1,0:T(8,128)S(1)} %concatenate.21.table, s32[1,8192]{1,0:T(1,128)S(1)} %bitcast.80, bf16[2,1,64,128,128]{4,3,2,1,0:T(8,128)(2,1)} %pages.1), custom_call_target="tpu_custom_call" | custom-call | tf_op jit(solution)/shard_map/attend/pallas_call | solution.py:167
  29.9 3.5 %all-to-all-start.1 = ((bf16[16,8,1024]{2,1,0:T(8,128)(2,1)}), bf16[16,8,1024]{2,1,0:T(8,128)(2,1)S(1)}, u32[]{:S(2)}, u32[]{:S(2)}) async-start(bf16[16,8,1024]{2,1,0:T(8,128)(2,1)} %attend.1), calls=%async_computation.1 | async-start | bytes 524288 | tf_op jit(solution)/shard_map/all_to_all | solution.py:336
  33.5 0.1 broadcast_select_fusion.1
  33.5 0.0 copy-start.3
  33.5 0.1 pad_maximum_fusion
  33.6 7.7 %all-to-all-done.1 = bf16[16,8,1024]{2,1,0:T(8,128)(2,1)S(1)} async-done(((bf16[16,8,1024]{2,1,0:T(8,128)(2,1)}), bf16[16,8,1024]{2,1,0:T(8,128)(2,1)S(1)}, u32[]{:S(2)}, u32[]{:S(2)}) %all-to-all-start.1) | async-done | bytes 262176 | tf_op jit(solution)/shard_map/all_to_all | solution.py:336
  41.3 1.0 convolution_convert_fusion
  42.3 8.2 %all-to-all-start.2 = ((bf16[8,16,512]{2,1,0:T(8,128)(2,1)}), bf16[8,16,512]{2,1,0:T(8,128)(2,1)S(1)}, u32[]{:S(2)}, u32[]{:S(2)}) async-start(bf16[8,16,512]{2,1,0:T(8,128)(2,1)} %bitcast.11), calls=%async_computation.2 | async-start | bytes 262144 | tf_op jit(solution)/shard_map/all_to_all | solution.py:347
  50.5 0.0 collective-permute-done
  50.5 7.9 %all-to-all-done.2 = bf16[8,16,512]{2,1,0:T(8,128)(2,1)S(1)} async-done(((bf16[8,16,512]{2,1,0:T(8,128)(2,1)}), bf16[8,16,512]{2,1,0:T(8,128)(2,1)S(1)}, u32[]{:S(2)}, u32[]{:S(2)}) %all-to-all-start.2) | async-done | bytes 131104 | tf_op jit(solution)/shard_map/all_to_all | solution.py:347
  58.4 0.7 broadcast_in_dim.54
  59.2 6.3 %all-to-all-start.3 = ((bf16[16,16,512]{2,1,0:T(8,128)(2,1)}), bf16[16,16,512]{2,1,0:T(8,128)(2,1)S(1)}, u32[]{:S(2)}, u32[]{:S(2)}) async-start(bf16[16,16,512]{2,1,0:T(8,128)(2,1)} %broadcast_in_dim.54), calls=%async_computation.3 | async-start | bytes 524288 | tf_op jit(solution)/shard_map/all_to_all | solution.py:37
  65.4 0.1 pad_add_fusion.place
  65.5 11.7 %all-to-all-done.3 = bf16[16,16,512]{2,1,0:T(8,128)(2,1)S(1)} async-done(((bf16[16,16,512]{2,1,0:T(8,128)(2,1)}), bf16[16,16,512]{2,1,0:T(8,128)(2,1)S(1)}, u32[]{:S(2)}, u32[]{:S(2)}) %all-to-all-start.3) | async-done | bytes 262176 | tf_op jit(solution)/shard_map/all_to_all | solution.py:37
  77.2 4.7 %head_partials.1 = (bf16[4,136,384]{2,1,0:T(8,128)(2,1)S(1)}, bf16[4,136,384]{2,1,0:T(8,128)(2,1)S(1)}, bf16[4,136,384]{2,1,0:T(8,128)(2,1)S(1)}, bf16[4,136,384...) custom-call(s32[3]{0:T(128)S(1)} %pad_add_fusion.place, ...), custom_call_target="tpu_custom_call" | custom-call | tf_op jit(solution)/shard_map/head_partials/pallas_call | solution.py:256
  81.9 0.1 collective-permute-start.3
  82.0 1.9 %collective-permute-start.4 = (bf16[4,136,384]{2,1,0:T(8,128)(2,1)S(1)}, bf16[4,136,384]{2,1,0:T(8,128)(2,1)S(1)}, u32[]{:S(2)}, u32[]{:S(2)}) collective-permute-start(bf16[4,136,384]{2,1,0:T(8,128)(2,1)S(1)} %get-tuple-element.12), channel_id=1, source_target_pairs={{0,16},{8,24},{16,0},{24,8},{1,17},{9,25},{17,1},{25,9},{2,18},{10... | collective-permute-start | bytes 1253384 | tf_op jit(solution)/shard_map/ppermute | solution.py:42
  83.9 1.1 collective-permute-start.5
  85.1 0.1 collective-permute-start.9
  85.2 1.7 %collective-permute-start.10 = (bf16[4,136,384]{2,1,0:T(8,128)(2,1)S(1)}, bf16[4,136,384]{2,1,0:T(8,128)(2,1)S(1)}, u32[]{:S(2)}, u32[]{:S(2)}) collective-permute-start(bf16[4,136,384]{2,1,0:T(8,128)(2,1)S(1)} %get-tuple-element.16), channel_id=1, source_target_pairs={{0,4},{2,6},{4,0},{6,2},{1,5},{3,7},{5,1},{7,3},{8,12},{10,14},{12... | collective-permute-start | bytes 1253384 | tf_op jit(solution)/shard_map/ppermute | solution.py:42
  86.9 16.8 %collective-permute-done.3 = bf16[4,136,384]{2,1,0:T(8,128)(2,1)S(1)} collective-permute-done((bf16[4,136,384]{2,1,0:T(8,128)(2,1)S(1)}, bf16[4,136,384]{2,1,0:T(8,128)(2,1)S(1)}, u32[]{:S(2)}, u32[]{:S(2)}) %collective-permute-start.3) | collective-permute-done | bytes 417824 | tf_op jit(solution)/shard_map/ppermute | solution.py:42
  103.7 0.5 collective-permute-start.11
  104.2 0.0 collective-permute-done.5
  104.3 0.2 add_convert_fusion.1
  104.5 1.2 collective-permute-start.6
  105.7 1.7 %collective-permute-start.8 = (bf16[136,384]{1,0:T(8,128)(2,1)S(1)}, bf16[136,384]{1,0:T(8,128)(2,1)S(1)}, u32[]{:S(2)}, u32[]{:S(2)}) collective-permute-start(bf16[136,384]{1,0:T(8,128)(2,1)S(1)} %get-tuple-element.25), channel_id=1, source_target_pairs={{0,6},{2,0},{4,2},{6,4},{1,7},{3,1},{5,3},{7,5},{8,14},{10,8},{12,... | collective-permute-start | bytes 313352 | tf_op jit(solution)/shard_map/ppermute | solution.py:42
  107.5 0.1 collective-permute-start.7
  107.6 7.0 %collective-permute-done.11 = bf16[4,136,384]{2,1,0:T(8,128)(2,1)S(1)} collective-permute-done((bf16[4,136,384]{2,1,0:T(8,128)(2,1)S(1)}, bf16[4,136,384]{2,1,0:T(8,128)(2,1)S(1)}, u32[]{:S(2)}, u32[]{:S(2)}) %collective-permute-start.11) | collective-permute-done | bytes 417824 | tf_op jit(solution)/shard_map/ppermute | solution.py:42
  114.6 0.2 add_convert_fusion
  114.9 0.1 collective-permute-start.12
  115.0 2.7 %collective-permute-start.14 = (bf16[136,384]{1,0:T(8,128)(2,1)S(1)}, bf16[136,384]{1,0:T(8,128)(2,1)S(1)}, u32[]{:S(2)}, u32[]{:S(2)}) collective-permute-start(bf16[136,384]{1,0:T(8,128)(2,1)S(1)} %get-tuple-element.28), channel_id=1, source_target_pairs={{0,24},{8,0},{16,8},{24,16},{1,25},{9,1},{17,9},{25,17},{2,26},{10... | collective-permute-start | bytes 313352 | tf_op jit(solution)/shard_map/ppermute | solution.py:42
  117.6 0.0 collective-permute-done.6
  117.6 0.0 collective-permute-start.13
  117.6 0.0 collective-permute-done.8
  117.7 0.1 fusion.4
  117.7 0.1 slice_multiply_fusion.1
  117.8 1.9 %collective-permute-done.12 = bf16[136,384]{1,0:T(8,128)(2,1)S(1)} collective-permute-done((bf16[136,384]{1,0:T(8,128)(2,1)S(1)}, bf16[136,384]{1,0:T(8,128)(2,1)S(1)}, u32[]{:S(2)}, u32[]{:S(2)}) %collective-permute-start.12) | collective-permute-done | bytes 104480 | tf_op jit(solution)/shard_map/ppermute | solution.py:42
  119.7 0.7 collective-permute-done.14
  120.4 2.4 %collective-permute-done.13 = bf16[136,384]{1,0:T(8,128)(2,1)S(1)} collective-permute-done((bf16[136,384]{1,0:T(8,128)(2,1)S(1)}, bf16[136,384]{1,0:T(8,128)(2,1)S(1)}, u32[]{:S(2)}, u32[]{:S(2)}) %collective-permute-start.13) | collective-permute-done | bytes 104480 | tf_op jit(solution)/shard_map/ppermute | solution.py:42
  122.8 0.1 fusion.2
  122.9 0.1 slice_multiply_fusion
  122.9 0.1 fusion.23
  123.1 0.0 copy-start
  123.1 0.2 exponential_reduce_fusion
  123.3 14.4 %all_to_all.30 = f32[32,2,256]{2,1,0:T(2,128)S(1)} all-to-all(f32[32,2,256]{2,1,0:T(2,128)S(1)} %broadcast_in_dim.55), channel_id=1, replica_groups=mesh['batch'=8,'mp_0'=4,'mp_1'=4,'mp_2'=2] {'mp_0','mp_1','mp_2'}, dimensions={0} | all-to-all | bytes 131072 | tf_op jit(solution)/shard_map/all_to_all | solution.py:37
  137.8 0.1 slice_reduce_fusion.1
  137.9 9.0 %all_to_all.31 = f32[8,2,256]{2,1,0:T(2,128)S(1)} all-to-all(f32[8,2,256]{2,1,0:T(2,128)S(1)} %broadcast_in_dim.56), channel_id=1, replica_groups=mesh['batch'=8,'mp_0'=4,'mp_1'=4,'mp_2'=2] {'batch'}, dimensions={0} | all-to-all | bytes 32768 | tf_op jit(solution)/shard_map/all_to_all | solution.py:37
  147.0 0.6 log_add_fusion
  (34 shorter events, 0.3 us)
Async XLA Ops:
  0.6 13.0 %copy-start.5 = (s32[8]{0:T(128)S(1)}, s32[8]{0:T(128)}, u32[]{:S(2)}) copy-start(s32[8]{0:T(128)} %param.17) | copy-start | bytes 100
  0.6 13.3 %copy-start.2 = (f32[1024]{0:T(1024)S(1)}, f32[1024]{0:T(1024)}, u32[]{:S(2)}) copy-start(f32[1024]{0:T(1024)} %param.12) | copy-start | bytes 12292
  0.7 13.4 %copy-start.4 = (s32[8,24]{1,0:T(8,128)S(1)}, s32[8,24]{1,0:T(8,128)}, u32[]{:S(2)}) copy-start(s32[8,24]{1,0:T(8,128)} %param.16) | copy-start | bytes 2308
  0.7 76.5 %collective-permute-start.2 = (bf16[256,12288]{1,0:T(8,128)(2,1)}, bf16[256,12288]{1,0:T(8,128)(2,1)}, u32[]{:S(2)}, u32[]{:S(2)}) collective-permute-start(bf16[256,12288]{1,0:T(8,128)(2,1)} %near_weight.1), channel_id=1, source_target_pairs={{0,1},{1,0},{2,3},{3,2},{4,5},{5,4},{6,7},{7,6},{8,9},{9,8},{10,11... | collective-permute-start | bytes 18874376 | tf_op jit(solution)/shard_map/ppermute | solution.py:42
  5.3 45.1 %collective-permute-start = (f32[17,256]{1,0:T(8,128)S(1)}, f32[17,256]{1,0:T(8,128)S(1)}, u32[]{:S(2)}, u32[]{:S(2)}) collective-permute-start(f32[17,256]{1,0:T(8,128)S(1)} %pad_maximum_fusion.2), channel_id=1, source_target_pairs={{0,1},{1,0},{2,3},{3,2},{4,5},{5,4},{6,7},{7,6},{8,9},{9,8},{10,11... | collective-permute-start | bytes 52232 | tf_op jit(solution)/shard_map/ppermute | solution.py:42
  5.4 28.0 %collective-permute-start.1 = (bf16[1024,256]{1,0:T(8,128)(2,1)}, bf16[1024,256]{1,0:T(8,128)(2,1)S(1)}, u32[]{:S(2)}, u32[]{:S(2)}) collective-permute-start(bf16[1024,256]{1,0:T(8,128)(2,1)} %param.14), channel_id=1, source_target_pairs={{0,1},{1,0},{2,3},{3,2},{4,5},{5,4},{6,7},{7,6},{8,9},{9,8},{10,11... | collective-permute-start | bytes 1572872 | tf_op jit(solution)/shard_map/ppermute | solution.py:42
  8.1 17.8 %all-to-all-start = ((bf16[32,8,1152]{2,1,0:T(8,128)(2,1)}), bf16[32,8,1152]{2,1,0:T(8,128)(2,1)S(1)}, u32[]{:S(2)}, u32[]{:S(2)}) async-start(bf16[32,8,1152]{2,1,0:T(8,128)(2,1)} %bitcast.8), calls=%async_computation | async-start | bytes 1179648 | tf_op jit(solution)/shard_map/all_to_all | solution.py:326
  26.0 7.5 %copy-start.1 = (bf16[1024,256]{1,0:T(8,128)(2,1)S(1)}, bf16[1024,256]{1,0:T(8,128)(2,1)}, u32[]{:S(2)}) copy-start(bf16[1024,256]{1,0:T(8,128)(2,1)} %param.14) | copy-start | bytes 1572868
  29.9 11.4 %all-to-all-start.1 = ((bf16[16,8,1024]{2,1,0:T(8,128)(2,1)}), bf16[16,8,1024]{2,1,0:T(8,128)(2,1)S(1)}, u32[]{:S(2)}, u32[]{:S(2)}) async-start(bf16[16,8,1024]{2,1,0:T(8,128)(2,1)} %attend.1), calls=%async_computation.1 | async-start | bytes 524288 | tf_op jit(solution)/shard_map/all_to_all | solution.py:336
  33.5 16.9 %copy-start.3 = (f32[256]{0:T(256)S(1)}, f32[256]{0:T(256)}, u32[]{:S(2)}) copy-start(f32[256]{0:T(256)} %param.18) | copy-start | bytes 3076
  42.3 16.1 %all-to-all-start.2 = ((bf16[8,16,512]{2,1,0:T(8,128)(2,1)}), bf16[8,16,512]{2,1,0:T(8,128)(2,1)S(1)}, u32[]{:S(2)}, u32[]{:S(2)}) async-start(bf16[8,16,512]{2,1,0:T(8,128)(2,1)} %bitcast.11), calls=%async_computation.2 | async-start | bytes 262144 | tf_op jit(solution)/shard_map/all_to_all | solution.py:347
  59.2 18.0 %all-to-all-start.3 = ((bf16[16,16,512]{2,1,0:T(8,128)(2,1)}), bf16[16,16,512]{2,1,0:T(8,128)(2,1)S(1)}, u32[]{:S(2)}, u32[]{:S(2)}) async-start(bf16[16,16,512]{2,1,0:T(8,128)(2,1)} %broadcast_in_dim.54), calls=%async_computation.3 | async-start | bytes 524288 | tf_op jit(solution)/shard_map/all_to_all | solution.py:37
  81.9 21.8 %collective-permute-start.3 = (bf16[4,136,384]{2,1,0:T(8,128)(2,1)S(1)}, bf16[4,136,384]{2,1,0:T(8,128)(2,1)S(1)}, u32[]{:S(2)}, u32[]{:S(2)}) collective-permute-start(bf16[4,136,384]{2,1,0:T(8,128)(2,1)S(1)} %get-tuple-element.11), channel_id=1, source_target_pairs={{0,8},{8,16},{16,24},{24,0},{1,9},{9,17},{17,25},{25,1},{2,10},{10... | collective-permute-start | bytes 1253384 | tf_op jit(solution)/shard_map/ppermute | solution.py:42
  82.0 22.2 %collective-permute-start.4 = (bf16[4,136,384]{2,1,0:T(8,128)(2,1)S(1)}, bf16[4,136,384]{2,1,0:T(8,128)(2,1)S(1)}, u32[]{:S(2)}, u32[]{:S(2)}) collective-permute-start(bf16[4,136,384]{2,1,0:T(8,128)(2,1)S(1)} %get-tuple-element.12), channel_id=1, source_target_pairs={{0,16},{8,24},{16,0},{24,8},{1,17},{9,25},{17,1},{25,9},{2,18},{10... | collective-permute-start | bytes 1253384 | tf_op jit(solution)/shard_map/ppermute | solution.py:42
  83.9 20.3 %collective-permute-start.5 = (bf16[4,136,384]{2,1,0:T(8,128)(2,1)S(1)}, bf16[4,136,384]{2,1,0:T(8,128)(2,1)S(1)}, u32[]{:S(2)}, u32[]{:S(2)}) collective-permute-start(bf16[4,136,384]{2,1,0:T(8,128)(2,1)S(1)} %get-tuple-element.13), channel_id=1, source_target_pairs={{0,24},{8,0},{16,8},{24,16},{1,25},{9,1},{17,9},{25,17},{2,26},{10... | collective-permute-start | bytes 1253384 | tf_op jit(solution)/shard_map/ppermute | solution.py:42
  85.1 22.4 %collective-permute-start.9 = (bf16[4,136,384]{2,1,0:T(8,128)(2,1)S(1)}, bf16[4,136,384]{2,1,0:T(8,128)(2,1)S(1)}, u32[]{:S(2)}, u32[]{:S(2)}) collective-permute-start(bf16[4,136,384]{2,1,0:T(8,128)(2,1)S(1)} %get-tuple-element.15), channel_id=1, source_target_pairs={{0,2},{2,4},{4,6},{6,0},{1,3},{3,5},{5,7},{7,1},{8,10},{10,12},{12... | collective-permute-start | bytes 1253384 | tf_op jit(solution)/shard_map/ppermute | solution.py:42
  85.2 22.4 %collective-permute-start.10 = (bf16[4,136,384]{2,1,0:T(8,128)(2,1)S(1)}, bf16[4,136,384]{2,1,0:T(8,128)(2,1)S(1)}, u32[]{:S(2)}, u32[]{:S(2)}) collective-permute-start(bf16[4,136,384]{2,1,0:T(8,128)(2,1)S(1)} %get-tuple-element.16), channel_id=1, source_target_pairs={{0,4},{2,6},{4,0},{6,2},{1,5},{3,7},{5,1},{7,3},{8,12},{10,14},{12... | collective-permute-start | bytes 1253384 | tf_op jit(solution)/shard_map/ppermute | solution.py:42
  103.7 10.9 %collective-permute-start.11 = (bf16[4,136,384]{2,1,0:T(8,128)(2,1)S(1)}, bf16[4,136,384]{2,1,0:T(8,128)(2,1)S(1)}, u32[]{:S(2)}, u32[]{:S(2)}) collective-permute-start(bf16[4,136,384]{2,1,0:T(8,128)(2,1)S(1)} %get-tuple-element.17), channel_id=1, source_target_pairs={{0,6},{2,0},{4,2},{6,4},{1,7},{3,1},{5,3},{7,5},{8,14},{10,8},{12,... | collective-permute-start | bytes 1253384 | tf_op jit(solution)/shard_map/ppermute | solution.py:42
  104.5 13.1 %collective-permute-start.6 = (bf16[136,384]{1,0:T(8,128)(2,1)S(1)}, bf16[136,384]{1,0:T(8,128)(2,1)S(1)}, u32[]{:S(2)}, u32[]{:S(2)}) collective-permute-start(bf16[136,384]{1,0:T(8,128)(2,1)S(1)} %get-tuple-element.24), channel_id=1, source_target_pairs={{0,2},{2,4},{4,6},{6,0},{1,3},{3,5},{5,7},{7,1},{8,10},{10,12},{12... | collective-permute-start | bytes 313352 | tf_op jit(solution)/shard_map/ppermute | solution.py:42
  105.7 11.9 %collective-permute-start.8 = (bf16[136,384]{1,0:T(8,128)(2,1)S(1)}, bf16[136,384]{1,0:T(8,128)(2,1)S(1)}, u32[]{:S(2)}, u32[]{:S(2)}) collective-permute-start(bf16[136,384]{1,0:T(8,128)(2,1)S(1)} %get-tuple-element.25), channel_id=1, source_target_pairs={{0,6},{2,0},{4,2},{6,4},{1,7},{3,1},{5,3},{7,5},{8,14},{10,8},{12,... | collective-permute-start | bytes 313352 | tf_op jit(solution)/shard_map/ppermute | solution.py:42
  107.5 10.2 %collective-permute-start.7 = (bf16[136,384]{1,0:T(8,128)(2,1)S(1)}, bf16[136,384]{1,0:T(8,128)(2,1)S(1)}, u32[]{:S(2)}, u32[]{:S(2)}) collective-permute-start(bf16[136,384]{1,0:T(8,128)(2,1)S(1)} %get-tuple-element.26), channel_id=1, source_target_pairs={{0,4},{2,6},{4,0},{6,2},{1,5},{3,7},{5,1},{7,3},{8,12},{10,14},{12... | collective-permute-start | bytes 313352 | tf_op jit(solution)/shard_map/ppermute | solution.py:42
  114.9 4.8 %collective-permute-start.12 = (bf16[136,384]{1,0:T(8,128)(2,1)S(1)}, bf16[136,384]{1,0:T(8,128)(2,1)S(1)}, u32[]{:S(2)}, u32[]{:S(2)}) collective-permute-start(bf16[136,384]{1,0:T(8,128)(2,1)S(1)} %get-tuple-element.27), channel_id=1, source_target_pairs={{0,8},{8,16},{16,24},{24,0},{1,9},{9,17},{17,25},{25,1},{2,10},{10... | collective-permute-start | bytes 313352 | tf_op jit(solution)/shard_map/ppermute | solution.py:42
  115.0 5.4 %collective-permute-start.14 = (bf16[136,384]{1,0:T(8,128)(2,1)S(1)}, bf16[136,384]{1,0:T(8,128)(2,1)S(1)}, u32[]{:S(2)}, u32[]{:S(2)}) collective-permute-start(bf16[136,384]{1,0:T(8,128)(2,1)S(1)} %get-tuple-element.28), channel_id=1, source_target_pairs={{0,24},{8,0},{16,8},{24,16},{1,25},{9,1},{17,9},{25,17},{2,26},{10... | collective-permute-start | bytes 313352 | tf_op jit(solution)/shard_map/ppermute | solution.py:42
  117.6 5.1 %collective-permute-start.13 = (bf16[136,384]{1,0:T(8,128)(2,1)S(1)}, bf16[136,384]{1,0:T(8,128)(2,1)S(1)}, u32[]{:S(2)}, u32[]{:S(2)}) collective-permute-start(bf16[136,384]{1,0:T(8,128)(2,1)S(1)} %get-tuple-element.29), channel_id=1, source_target_pairs={{0,16},{8,24},{16,0},{24,8},{1,17},{9,25},{17,1},{25,9},{2,18},{10... | collective-permute-start | bytes 313352 | tf_op jit(solution)/shard_map/ppermute | solution.py:42
  123.1 24.5 %copy-start = (f32[256,384]{1,0:T(8,128)}, f32[256,384]{1,0:T(8,128)S(1)}, u32[]{:S(2)}) copy-start(f32[256,384]{1,0:T(8,128)S(1)} %get-tuple-element.21) | copy-start | bytes 1179652
